TPU v7x, 256 devices: a whole 4x4x8 slice. The times are simulated.
256 devices in a mesh: batch: 32 (over y, x, core), rows: 8 (over z).
Axes of the slice: x: 4, y: 4, z: 8, core: 2. Of those that a mesh axis runs over, the one named last changes fastest.
Arguments:
- fine_level: bfloat16 [32, 64, 192, 384], P('batch', 'rows'), may hold values from -40 to 40
- middle_level: bfloat16 [32, 32, 96, 384], P('batch', 'rows'), may hold values from -40 to 40
- coarse_level: bfloat16 [32, 16, 48, 384], P('batch', 'rows'), may hold values from -40 to 40
- two_input_weights: float32 [2, 3, 2], replicated, may hold values from 0.5 to 2
- three_input_weights: float32 [2, 3], replicated, may hold values from 0.5 to 2
- depthwise: bfloat16 [2, 4, 3, 3, 384], replicated, may hold values from -2 to 2
- pointwise: bfloat16 [2, 4, 384, 384], replicated, may hold values from -0.3125 to 0.3125
- bn_gain: float32 [2, 4, 384], replicated, may hold values from 0.5 to 1.5
- bn_bias: float32 [2, 4, 384], replicated, may hold values from -3 to 3
Outputs:
- fine_result: bfloat16 [32, 64, 192, 384], P('batch', 'rows')
- middle_result: bfloat16 [32, 32, 96, 384], P('batch', 'rows')
- coarse_result: bfloat16 [32, 16, 48, 384], P('batch', 'rows')
All inputs are finite; a program needn't handle non-finite values.
Results may differ from a plain program's by a relative error of at most 0.025.
Values may be sent and summed in bfloat16 or wider, within the bound.
No kernel may reach another device: no remote copies, remote signals or barrier semaphores. Data moves between devices by JAX's collectives and lax.ppermute only.
A program may use at most 64 MiB of HBM per device.

v0:
```python
import jax
import jax.numpy as jnp
from jax import lax
from jax.sharding import Mesh
from jax.sharding import PartitionSpec as P

LAYERS = 2
BATCH = ("batch_0", "batch_1", "batch_2")


def from_behind(block, axis, distance):
    devices = range(lax.axis_size(axis))
    route = [(i - distance, i) for i in devices if i - distance in devices]
    return lax.ppermute(block, axis, route)


def sent_to_all(value, axis):
    copies = jnp.broadcast_to(value, (lax.axis_size(axis), *value.shape))
    return lax.all_to_all(copies, axis, split_axis=0, concat_axis=0, tiled=True)


def over_copies(value, axis):
    return sent_to_all(value, axis).sum(axis=0)


def one_axis_at_a_time(value, axes):
    far, near = axes
    return over_copies(over_copies(value, near), far)


def packed_total(arrays, axis):
    vector, at, finished = (jnp.concatenate([a.reshape(-1) for a in arrays]), 0, [])
    total = one_axis_at_a_time(vector, axis)
    for a in arrays:
        finished.append(total[at : at + a.size].reshape(a.shape))
        at += a.size
    return tuple(finished)


def extended_2(block, sides, width):
    for axis, dim in sides:
        count = lax.axis_size(axis)
        forward = [(i, i + 1) for i in range(count - 1)]
        backward = [(target, source) for source, target in forward]
        low = lax.ppermute(
            lax.slice_in_dim(block, block.shape[dim] - width, None, axis=dim), axis, forward
        )
        high = lax.ppermute(lax.slice_in_dim(block, 0, width, axis=dim), axis, backward)
        block = jnp.concatenate([low, block, high], axis=dim)
    return block


def upsample(feature_maps):
    return jnp.repeat(jnp.repeat(feature_maps, 2, axis=1), 2, axis=2)


def reduce_resolution(feature_maps):
    beneath = from_behind(feature_maps[:, :1], "rows", -1)
    lowest = jnp.array(-jnp.inf, feature_maps.dtype)
    at_bottom = lax.axis_index("rows") == lax.axis_size("rows") - 1
    beneath = jnp.where(at_bottom, lowest, beneath)
    extended = jnp.concatenate([feature_maps, beneath], axis=1)
    padded = jnp.pad(extended, ((0, 0), (0, 0), (0, 1), (0, 0)), constant_values=lowest)
    return lax.reduce_window(padded, lowest, lax.max, (1, 3, 3, 1), (1, 2, 2, 1), "VALID")


def weighted_join_activate(inputs_list, weights):
    weight_sum = jnp.sum(weights) + 0.0001
    running = weights[0] * inputs_list[0].astype(jnp.float32)
    for position in range(1, len(inputs_list)):
        running = running + weights[position] * inputs_list[position].astype(jnp.float32)
    return jax.nn.silu(running / weight_sum).astype(jnp.bfloat16)


def separable(extended, kernel, projection):
    padded = jnp.pad(extended, ((0, 0), (0, 0), (1, 1), (0, 0)))
    height = extended.shape[1] - 2
    width = extended.shape[2]
    running = jnp.zeros((extended.shape[0], height, width, extended.shape[3]), jnp.float32)
    for row_tap in range(3):
        for col_tap in range(3):
            window = padded[:, row_tap : row_tap + height, col_tap : col_tap + width, :]
            running = running + window.astype(jnp.float32) * kernel[row_tap, col_tap].astype(
                jnp.float32
            )
    spatial = running.astype(jnp.bfloat16)
    projected = jnp.dot(
        spatial.reshape(-1, spatial.shape[-1]), projection, preferred_element_type=jnp.float32
    )
    return projected.reshape(spatial.shape)


def normalize(projected, gain, offset):
    count = float(
        projected.shape[0]
        * projected.shape[1]
        * projected.shape[2]
        * lax.axis_size(BATCH)
        * lax.axis_size("rows")
    )
    totals, squares = packed_total(
        (jnp.sum(projected, axis=(0, 1, 2)), jnp.sum(projected * projected, axis=(0, 1, 2))),
        (("batch_0", "batch_1"), ("batch_2", "rows")),
    )
    center = totals / count
    spread = squares / count - center * center
    centered = projected - center
    return (centered * lax.rsqrt(spread + 1e-05) * gain + offset).astype(jnp.bfloat16)


def node(activated, kernel, projection, gain, offset):
    extended = extended_2(activated, (("rows", 1),), 1)
    return normalize(separable(extended, kernel, projection), gain, offset)


def body(
    fine_level,
    middle_level,
    coarse_level,
    two_input_weights,
    three_input_weights,
    depthwise,
    pointwise,
    bn_gain,
    bn_bias,
):
    fine, middle_grid, coarse_grid = (fine_level, middle_level, coarse_level)
    for bidirectional_layer in range(LAYERS):

        def run_layer_pair(index, activated):
            return node(
                activated,
                depthwise[bidirectional_layer, index],
                pointwise[bidirectional_layer, index],
                bn_gain[bidirectional_layer, index],
                bn_bias[bidirectional_layer, index],
            )

        downward_middle = run_layer_pair(
            0,
            weighted_join_activate(
                [middle_grid, upsample(coarse_grid)], two_input_weights[bidirectional_layer, 0]
            ),
        )
        updated_fine = run_layer_pair(
            1,
            weighted_join_activate(
                [fine, upsample(downward_middle)], two_input_weights[bidirectional_layer, 1]
            ),
        )
        updated_middle = run_layer_pair(
            2,
            weighted_join_activate(
                [middle_grid, downward_middle, reduce_resolution(updated_fine)],
                three_input_weights[bidirectional_layer],
            ),
        )
        updated_coarse = run_layer_pair(
            3,
            weighted_join_activate(
                [coarse_grid, reduce_resolution(updated_middle)],
                two_input_weights[bidirectional_layer, 2],
            ),
        )
        fine, middle_grid, coarse_grid = (updated_fine, updated_middle, updated_coarse)
    return (fine, middle_grid, coarse_grid)


def solution(mesh):
    split = Mesh(
        mesh.devices.reshape(4, 4, 2, mesh.shape["rows"]), ("batch_0", "batch_1", "batch_2", "rows")
    )
    in_specs = (
        P(BATCH, "rows", None, None),
        P(BATCH, "rows", None, None),
        P(BATCH, "rows", None, None),
        P(),
        P(),
        P(),
        P(),
        P(),
        P(),
    )
    out_specs = (
        P(BATCH, "rows", None, None),
        P(BATCH, "rows", None, None),
        P(BATCH, "rows", None, None),
    )
    return jax.shard_map(body, mesh=split, in_specs=in_specs, out_specs=out_specs, check_vma=False)
```

profile of v0, /device:TPU:1, one launch (start us, length us, event | category | flops | bytes accessed | tf_op | source)
XLA Modules:
  0.0 369.2 jit_solution(15090444081342591841)
XLA Ops:
  7.6 4.4 %collective-permute-start = (bf16[1,1,96,384]{3,2,1,0:T(8,128)(2,1)S(1)}, bf16[1,1,96,384]{3,2,1,0:T(8,128)(2,1)S(1)}, u32[]{:S(2)}, u32[]{:S(2)}) collective-permute-start(bf16[1,1,96,384]{3,2,1,0:T(8,128)(2,1)S(1)} %get-tuple-element.125), channel_id=1, source_target_pairs={{0,1},{1,2},{2,3},{3,4},{4,5},{5,6},{6,7},{8,9},{9,10},{10,11},{11... | collective-permute-start | bytes 221192 | tf_op jit(solution)/shard_map/ppermute | solution.py:45
  14.1 3.2 collective-permute-done.1
  19.2 17.1 %all_to_all.96 = f32[16,1,768]{2,1,0:T(1,128)S(1)} all-to-all(f32[16,1,768]{2,1,0:T(1,128)S(1)} %broadcast_in_dim.60), channel_id=1, replica_groups=mesh['batch_0'=4,'batch_1'=4,'batch_2'=2,'rows'=8] {'batch_2','rows'}, dimensions={0} | all-to-all | bytes 98304 | tf_op jit(solution)/shard_map/all_to_all | solution.py:19
  37.1 6.8 %all-to-all-start.1 = ((f32[16,1,768]{2,1,0:T(1,128)}), f32[16,1,768]{2,1,0:T(1,128)S(1)}, u32[]{:S(2)}, u32[]{:S(2)}) async-start(f32[16,1,768]{2,1,0:T(1,128)} %broadcast_in_dim.61), calls=%async_computation.1 | async-start | bytes 98304 | tf_op jit(solution)/shard_map/all_to_all | solution.py:19
  45.2 5.1 %all-to-all-done.1 = f32[16,1,768]{2,1,0:T(1,128)S(1)} async-done(((f32[16,1,768]{2,1,0:T(1,128)}), f32[16,1,768]{2,1,0:T(1,128)S(1)}, u32[]{:S(2)}, u32[]{:S(2)}) %all-to-all-start.1) | async-done | bytes 49184 | tf_op jit(solution)/shard_map/all_to_all | solution.py:19
  53.5 3.2 mul.1426
  58.1 2.6 collective-permute-start.2
  62.8 3.8 %collective-permute-done.3 = bf16[1,1,192,384]{3,2,1,0:T(8,128)(2,1)S(1)} collective-permute-done((bf16[1,1,192,384]{3,2,1,0:T(8,128)(2,1)S(1)}, bf16[1,1,192,384]{3,2,1,0:T(8,128)(2,1)S(1)}, u32[]{:S(2)}, u32[]{:S(2)}) %collective-permute-start.3) | collective-permute-done | bytes 147488 | tf_op jit(solution)/shard_map/ppermute | solution.py:48
  67.1 2.4 add_convert_fusion.3
  71.4 13.5 %all_to_all.97 = f32[16,1,768]{2,1,0:T(1,128)S(1)} all-to-all(f32[16,1,768]{2,1,0:T(1,128)S(1)} %broadcast_in_dim.64), channel_id=1, replica_groups=mesh['batch_0'=4,'batch_1'=4,'batch_2'=2,'rows'=8] {'batch_2','rows'}, dimensions={0} | all-to-all | bytes 98304 | tf_op jit(solution)/shard_map/all_to_all | solution.py:19
  85.6 3.5 all-to-all-start.3
  89.7 5.8 %all-to-all-done.3 = f32[16,1,768]{2,1,0:T(1,128)S(1)} async-done(((f32[16,1,768]{2,1,0:T(1,128)}), f32[16,1,768]{2,1,0:T(1,128)S(1)}, u32[]{:S(2)}, u32[]{:S(2)}) %all-to-all-start.3) | async-done | bytes 49184 | tf_op jit(solution)/shard_map/all_to_all | solution.py:19
  108.4 3.5 multiply_convert_fusion.4
  111.9 2.7 collective-permute-start.5
  116.2 3.5 collective-permute-done.6
  121.7 15.1 %all_to_all.98 = f32[16,1,768]{2,1,0:T(1,128)S(1)} all-to-all(f32[16,1,768]{2,1,0:T(1,128)S(1)} %broadcast_in_dim.67), channel_id=1, replica_groups=mesh['batch_0'=4,'batch_1'=4,'batch_2'=2,'rows'=8] {'batch_2','rows'}, dimensions={0} | all-to-all | bytes 98304 | tf_op jit(solution)/shard_map/all_to_all | solution.py:19
  136.9 9.3 %all_to_all.99 = f32[16,1,768]{2,1,0:T(1,128)S(1)} all-to-all(f32[16,1,768]{2,1,0:T(1,128)S(1)} %broadcast_in_dim.68), channel_id=1, replica_groups=mesh['batch_0'=4,'batch_1'=4,'batch_2'=2,'rows'=8] {'batch_0','batch_1'}, dimensions={0} | all-to-all | bytes 98304 | tf_op jit(solution)/shard_map/all_to_all | solution.py:19
  148.4 3.2 collective-permute-done.7
  154.9 2.6 collective-permute-start.8
  159.0 3.3 collective-permute-done.9
  163.7 15.3 %all_to_all.100 = f32[16,1,768]{2,1,0:T(1,128)S(1)} all-to-all(f32[16,1,768]{2,1,0:T(1,128)S(1)} %broadcast_in_dim.70), channel_id=1, replica_groups=mesh['batch_0'=4,'batch_1'=4,'batch_2'=2,'rows'=8] {'batch_2','rows'}, dimensions={0} | all-to-all | bytes 98304 | tf_op jit(solution)/shard_map/all_to_all | solution.py:19
  179.7 3.5 all-to-all-start.7
  183.9 5.7 %all-to-all-done.7 = f32[16,1,768]{2,1,0:T(1,128)S(1)} async-done(((f32[16,1,768]{2,1,0:T(1,128)}), f32[16,1,768]{2,1,0:T(1,128)S(1)}, u32[]{:S(2)}, u32[]{:S(2)}) %all-to-all-start.7) | async-done | bytes 49184 | tf_op jit(solution)/shard_map/all_to_all | solution.py:19
  196.3 2.6 collective-permute-start.10
  200.4 3.7 %collective-permute-done.11 = bf16[1,1,96,384]{3,2,1,0:T(8,128)(2,1)S(1)} collective-permute-done((bf16[1,1,96,384]{3,2,1,0:T(8,128)(2,1)S(1)}, bf16[1,1,96,384]{3,2,1,0:T(8,128)(2,1)S(1)}, u32[]{:S(2)}, u32[]{:S(2)}) %collective-permute-start.11) | collective-permute-done | bytes 73760 | tf_op jit(solution)/shard_map/ppermute | solution.py:48
  206.9 13.2 %all_to_all.101 = f32[16,1,768]{2,1,0:T(1,128)S(1)} all-to-all(f32[16,1,768]{2,1,0:T(1,128)S(1)} %broadcast_in_dim.74), channel_id=1, replica_groups=mesh['batch_0'=4,'batch_1'=4,'batch_2'=2,'rows'=8] {'batch_2','rows'}, dimensions={0} | all-to-all | bytes 98304 | tf_op jit(solution)/shard_map/all_to_all | solution.py:19
  220.8 3.5 all-to-all-start.9
  224.9 5.8 %all-to-all-done.9 = f32[16,1,768]{2,1,0:T(1,128)S(1)} async-done(((f32[16,1,768]{2,1,0:T(1,128)}), f32[16,1,768]{2,1,0:T(1,128)S(1)}, u32[]{:S(2)}, u32[]{:S(2)}) %all-to-all-start.9) | async-done | bytes 49184 | tf_op jit(solution)/shard_map/all_to_all | solution.py:19
  234.9 4.1 %mul.1555 = f32[1,8,192,384]{3,2,1,0:T(8,128)} reshape(f32[8,96,2,384]{3,2,1,0:T(2,128)} %broadcast_in_dim.77) | data formatting | bytes 4718592 | tf_op jit(solution)/shard_map/mul | solution.py:71
  239.0 3.3 multiply_convert_fusion
  242.4 2.6 collective-permute-start.12
  247.1 3.8 %collective-permute-done.13 = bf16[1,1,192,384]{3,2,1,0:T(8,128)(2,1)S(1)} collective-permute-done((bf16[1,1,192,384]{3,2,1,0:T(8,128)(2,1)S(1)}, bf16[1,1,192,384]{3,2,1,0:T(8,128)(2,1)S(1)}, u32[]{:S(2)}, u32[]{:S(2)}) %collective-permute-start.13) | collective-permute-done | bytes 147488 | tf_op jit(solution)/shard_map/ppermute | solution.py:48
  251.3 2.4 add_convert_fusion.1
  253.8 3.3 fusion.118
  257.1 13.2 %all_to_all.102 = f32[16,1,768]{2,1,0:T(1,128)S(1)} all-to-all(f32[16,1,768]{2,1,0:T(1,128)S(1)} %broadcast_in_dim.78), channel_id=1, replica_groups=mesh['batch_0'=4,'batch_1'=4,'batch_2'=2,'rows'=8] {'batch_2','rows'}, dimensions={0} | all-to-all | bytes 98304 | tf_op jit(solution)/shard_map/all_to_all | solution.py:19
  271.0 3.5 all-to-all-start.11
  275.0 5.8 %all-to-all-done.11 = f32[16,1,768]{2,1,0:T(1,128)S(1)} async-done(((f32[16,1,768]{2,1,0:T(1,128)}), f32[16,1,768]{2,1,0:T(1,128)S(1)}, u32[]{:S(2)}, u32[]{:S(2)}) %all-to-all-start.11) | async-done | bytes 49184 | tf_op jit(solution)/shard_map/all_to_all | solution.py:19
  285.0 4.0 %collective-permute-done.14 = bf16[1,1,192,384]{3,2,1,0:T(8,128)(2,1)S(1)} collective-permute-done((bf16[1,1,192,384]{3,2,1,0:T(8,128)(2,1)S(1)}, bf16[1,1,192,384]{3,2,1,0:T(8,128)(2,1)S(1)}, u32[]{:S(2)}, u32[]{:S(2)}) %collective-permute-start.14) | collective-permute-done | bytes 147488 | tf_op jit(solution)/shard_map/ppermute | solution.py:14
  290.3 3.4 multiply_convert_fusion.2
  293.8 2.6 collective-permute-start.15
  298.6 2.9 collective-permute-done.16
  303.5 15.0 %all_to_all.103 = f32[16,1,768]{2,1,0:T(1,128)S(1)} all-to-all(f32[16,1,768]{2,1,0:T(1,128)S(1)} %broadcast_in_dim.80), channel_id=1, replica_groups=mesh['batch_0'=4,'batch_1'=4,'batch_2'=2,'rows'=8] {'batch_2','rows'}, dimensions={0} | all-to-all | bytes 98304 | tf_op jit(solution)/shard_map/all_to_all | solution.py:19
  318.6 9.3 %all_to_all.104 = f32[16,1,768]{2,1,0:T(1,128)S(1)} all-to-all(f32[16,1,768]{2,1,0:T(1,128)S(1)} %broadcast_in_dim.81), channel_id=1, replica_groups=mesh['batch_0'=4,'batch_1'=4,'batch_2'=2,'rows'=8] {'batch_0','batch_1'}, dimensions={0} | all-to-all | bytes 98304 | tf_op jit(solution)/shard_map/all_to_all | solution.py:19
  330.1 3.2 collective-permute-done.17
  335.0 2.6 collective-permute-start.18
  339.1 3.3 collective-permute-done.19
  343.8 15.3 %all_to_all.105 = f32[16,1,768]{2,1,0:T(1,128)S(1)} all-to-all(f32[16,1,768]{2,1,0:T(1,128)S(1)} %broadcast_in_dim.82), channel_id=1, replica_groups=mesh['batch_0'=4,'batch_1'=4,'batch_2'=2,'rows'=8] {'batch_2','rows'}, dimensions={0} | all-to-all | bytes 98304 | tf_op jit(solution)/shard_map/all_to_all | solution.py:19
  359.2 9.3 %all_to_all.106 = f32[16,1,768]{2,1,0:T(1,128)S(1)} all-to-all(f32[16,1,768]{2,1,0:T(1,128)S(1)} %broadcast_in_dim.83), channel_id=1, replica_groups=mesh['batch_0'=4,'batch_1'=4,'batch_2'=2,'rows'=8] {'batch_0','batch_1'}, dimensions={0} | all-to-all | bytes 98304 | tf_op jit(solution)/shard_map/all_to_all | solution.py:19
  (250 shorter events, 81.3 us)
Async XLA Ops:
  7.6 6.5 %collective-permute-start = (bf16[1,1,96,384]{3,2,1,0:T(8,128)(2,1)S(1)}, bf16[1,1,96,384]{3,2,1,0:T(8,128)(2,1)S(1)}, u32[]{:S(2)}, u32[]{:S(2)}) collective-permute-start(bf16[1,1,96,384]{3,2,1,0:T(8,128)(2,1)S(1)} %get-tuple-element.125), channel_id=1, source_target_pairs={{0,1},{1,2},{2,3},{3,4},{4,5},{5,6},{6,7},{8,9},{9,10},{10,11},{11... | collective-permute-start | bytes 221192 | tf_op jit(solution)/shard_map/ppermute | solution.py:45
  12.0 5.3 %collective-permute-start.1 = (bf16[1,1,96,384]{3,2,1,0:T(8,128)(2,1)S(1)}, bf16[1,1,96,384]{3,2,1,0:T(8,128)(2,1)S(1)}, u32[]{:S(2)}, u32[]{:S(2)}) collective-permute-start(bf16[1,1,96,384]{3,2,1,0:T(8,128)(2,1)S(1)} %get-tuple-element.126), channel_id=1, source_target_pairs={{1,0},{2,1},{3,2},{4,3},{5,4},{6,5},{7,6},{9,8},{10,9},{11,10},{12... | collective-permute-start | bytes 221192 | tf_op jit(solution)/shard_map/ppermute | solution.py:48
  14.0 29.8 %copy-start.39 = (f32[2,4,384]{2,1,0:T(4,128)S(1)}, f32[2,4,384]{2,1,0:T(4,128)}, u32[]{:S(2)}) copy-start(f32[2,4,384]{2,1,0:T(4,128)} %param.17) | copy-start | bytes 36868
  14.0 29.8 %copy-start.40 = (f32[2,4,384]{2,1,0:T(4,128)S(1)}, f32[2,4,384]{2,1,0:T(4,128)}, u32[]{:S(2)}) copy-start(f32[2,4,384]{2,1,0:T(4,128)} %param.16) | copy-start | bytes 36868
  19.2 32.0 %copy-start.1 = (f32[384,384]{1,0:T(8,128)}, f32[384,384]{1,0:T(8,128)S(1)}, u32[]{:S(2)}) copy-start(f32[384,384]{1,0:T(8,128)S(1)} %get-tuple-element.173) | copy-start | bytes 1769476
  37.1 13.2 %all-to-all-start.1 = ((f32[16,1,768]{2,1,0:T(1,128)}), f32[16,1,768]{2,1,0:T(1,128)S(1)}, u32[]{:S(2)}, u32[]{:S(2)}) async-start(f32[16,1,768]{2,1,0:T(1,128)} %broadcast_in_dim.61), calls=%async_computation.1 | async-start | bytes 98304 | tf_op jit(solution)/shard_map/all_to_all | solution.py:19
  58.1 4.7 %collective-permute-start.2 = (bf16[1,1,192,384]{3,2,1,0:T(8,128)(2,1)S(1)}, bf16[1,1,192,384]{3,2,1,0:T(8,128)(2,1)S(1)}, u32[]{:S(2)}, u32[]{:S(2)}) collective-permute-start(bf16[1,1,192,384]{3,2,1,0:T(8,128)(2,1)S(1)} %get-tuple-element.117), channel_id=1, source_target_pairs={{0,1},{1,2},{2,3},{3,4},{4,5},{5,6},{6,7},{8,9},{9,10},{10,11},{11... | collective-permute-start | bytes 442376 | tf_op jit(solution)/shard_map/ppermute | solution.py:45
  60.8 5.9 %collective-permute-start.3 = (bf16[1,1,192,384]{3,2,1,0:T(8,128)(2,1)S(1)}, bf16[1,1,192,384]{3,2,1,0:T(8,128)(2,1)S(1)}, u32[]{:S(2)}, u32[]{:S(2)}) collective-permute-start(bf16[1,1,192,384]{3,2,1,0:T(8,128)(2,1)S(1)} %get-tuple-element.118), channel_id=1, source_target_pairs={{1,0},{2,1},{3,2},{4,3},{5,4},{6,5},{7,6},{9,8},{10,9},{11,10},{12... | collective-permute-start | bytes 442376 | tf_op jit(solution)/shard_map/ppermute | solution.py:48
  85.6 9.9 %all-to-all-start.3 = ((f32[16,1,768]{2,1,0:T(1,128)}), f32[16,1,768]{2,1,0:T(1,128)S(1)}, u32[]{:S(2)}, u32[]{:S(2)}) async-start(f32[16,1,768]{2,1,0:T(1,128)} %broadcast_in_dim.65), calls=%async_computation.3 | async-start | bytes 98304 | tf_op jit(solution)/shard_map/all_to_all | solution.py:19
  97.9 6.2 %collective-permute-start.4 = (bf16[1,1,192,384]{3,2,1,0:T(8,128)(2,1)}, bf16[1,1,192,384]{3,2,1,0:T(8,128)(2,1)}, u32[]{:S(2)}, u32[]{:S(2)}) collective-permute-start(bf16[1,1,192,384]{3,2,1,0:T(8,128)(2,1)} %slice.1038), channel_id=1, source_target_pairs={{1,0},{2,1},{3,2},{4,3},{5,4},{6,5},{7,6},{9,8},{10,9},{11,10},{12... | collective-permute-start | bytes 442376 | tf_op jit(solution)/shard_map/ppermute | solution.py:14
  111.9 4.3 %collective-permute-start.5 = (bf16[1,1,96,384]{3,2,1,0:T(8,128)(2,1)S(1)}, bf16[1,1,96,384]{3,2,1,0:T(8,128)(2,1)S(1)}, u32[]{:S(2)}, u32[]{:S(2)}) collective-permute-start(bf16[1,1,96,384]{3,2,1,0:T(8,128)(2,1)S(1)} %get-tuple-element.123), channel_id=1, source_target_pairs={{0,1},{1,2},{2,3},{3,4},{4,5},{5,6},{6,7},{8,9},{9,10},{10,11},{11... | collective-permute-start | bytes 221192 | tf_op jit(solution)/shard_map/ppermute | solution.py:45
  114.6 5.1 %collective-permute-start.6 = (bf16[1,1,96,384]{3,2,1,0:T(8,128)(2,1)S(1)}, bf16[1,1,96,384]{3,2,1,0:T(8,128)(2,1)S(1)}, u32[]{:S(2)}, u32[]{:S(2)}) collective-permute-start(bf16[1,1,96,384]{3,2,1,0:T(8,128)(2,1)S(1)} %get-tuple-element.124), channel_id=1, source_target_pairs={{1,0},{2,1},{3,2},{4,3},{5,4},{6,5},{7,6},{9,8},{10,9},{11,10},{12... | collective-permute-start | bytes 221192 | tf_op jit(solution)/shard_map/ppermute | solution.py:48
  116.2 30.2 %copy-start.14 = (f32[384]{0:T(512)S(1)}, f32[384]{0:T(512)}, u32[]{:S(2)}) copy-start(f32[384]{0:T(512)} %get-tuple-element.192) | copy-start | bytes 4612
  120.3 33.4 %copy-start.5 = (bf16[1,2,48,384]{3,2,1,0:T(8,128)(2,1)S(1)}, bf16[1,2,48,384]{3,2,1,0:T(8,128)(2,1)}, u32[]{:S(2)}) copy-start(bf16[1,2,48,384]{3,2,1,0:T(8,128)(2,1)} %param.11) | copy-start | bytes 221188
  146.3 36.9 %copy-start.10 = (bf16[1,1,3,3,384]{4,1,3,2,0:T(2,128)(2,1)S(1)}, bf16[1,1,3,3,384]{4,1,3,2,0:T(2,128)(2,1)}, u32[]{:S(2)}) copy-start(bf16[1,1,3,3,384]{4,1,3,2,0:T(2,128)(2,1)} %get-tuple-element.132) | copy-start | bytes 20740
  146.3 36.9 %copy-start.11 = (bf16[1,1,3,3,384]{4,1,3,2,0:T(2,128)(2,1)S(1)}, bf16[1,1,3,3,384]{4,1,3,2,0:T(2,128)(2,1)}, u32[]{:S(2)}) copy-start(bf16[1,1,3,3,384]{4,1,3,2,0:T(2,128)(2,1)} %get-tuple-element.133) | copy-start | bytes 20740
  146.5 5.1 %collective-permute-start.7 = (bf16[1,1,96,384]{3,2,1,0:T(8,128)(2,1)S(1)}, bf16[1,1,96,384]{3,2,1,0:T(8,128)(2,1)S(1)}, u32[]{:S(2)}, u32[]{:S(2)}) collective-permute-start(bf16[1,1,96,384]{3,2,1,0:T(8,128)(2,1)S(1)} %slice.1056), channel_id=1, source_target_pairs={{1,0},{2,1},{3,2},{4,3},{5,4},{6,5},{7,6},{9,8},{10,9},{11,10},{12... | collective-permute-start | bytes 221192 | tf_op jit(solution)/shard_map/ppermute | solution.py:14
  154.9 4.0 %collective-permute-start.8 = (bf16[1,1,48,384]{3,2,1,0:T(8,128)(2,1)S(1)}, bf16[1,1,48,384]{3,2,1,0:T(8,128)(2,1)S(1)}, u32[]{:S(2)}, u32[]{:S(2)}) collective-permute-start(bf16[1,1,48,384]{3,2,1,0:T(8,128)(2,1)S(1)} %get-tuple-element.129), channel_id=1, source_target_pairs={{0,1},{1,2},{2,3},{3,4},{4,5},{5,6},{6,7},{8,9},{9,10},{10,11},{11... | collective-permute-start | bytes 110600 | tf_op jit(solution)/shard_map/ppermute | solution.py:45
  157.6 4.7 %collective-permute-start.9 = (bf16[1,1,48,384]{3,2,1,0:T(8,128)(2,1)S(1)}, bf16[1,1,48,384]{3,2,1,0:T(8,128)(2,1)S(1)}, u32[]{:S(2)}, u32[]{:S(2)}) collective-permute-start(bf16[1,1,48,384]{3,2,1,0:T(8,128)(2,1)S(1)} %get-tuple-element.130), channel_id=1, source_target_pairs={{1,0},{2,1},{3,2},{4,3},{5,4},{6,5},{7,6},{9,8},{10,9},{11,10},{12... | collective-permute-start | bytes 110600 | tf_op jit(solution)/shard_map/ppermute | solution.py:48
  158.9 35.4 %copy-start.16 = (f32[384]{0:T(512)S(1)}, f32[384]{0:T(512)}, u32[]{:S(2)}) copy-start(f32[384]{0:T(512)} %copy-done.15) | copy-start | bytes 4612
  159.0 35.3 %copy-start.18 = (f32[384]{0:T(512)S(1)}, f32[384]{0:T(512)}, u32[]{:S(2)}) copy-start(f32[384]{0:T(512)} %copy-done.17) | copy-start | bytes 4612
  179.7 9.9 %all-to-all-start.7 = ((f32[16,1,768]{2,1,0:T(1,128)}), f32[16,1,768]{2,1,0:T(1,128)S(1)}, u32[]{:S(2)}, u32[]{:S(2)}) async-start(f32[16,1,768]{2,1,0:T(1,128)} %broadcast_in_dim.71), calls=%async_computation.7 | async-start | bytes 98304 | tf_op jit(solution)/shard_map/all_to_all | solution.py:19
  196.3 4.0 %collective-permute-start.10 = (bf16[1,1,96,384]{3,2,1,0:T(8,128)(2,1)S(1)}, bf16[1,1,96,384]{3,2,1,0:T(8,128)(2,1)S(1)}, u32[]{:S(2)}, u32[]{:S(2)}) collective-permute-start(bf16[1,1,96,384]{3,2,1,0:T(8,128)(2,1)S(1)} %get-tuple-element.121), channel_id=1, source_target_pairs={{0,1},{1,2},{2,3},{3,4},{4,5},{5,6},{6,7},{8,9},{9,10},{10,11},{11... | collective-permute-start | bytes 221192 | tf_op jit(solution)/shard_map/ppermute | solution.py:45
  199.0 5.1 %collective-permute-start.11 = (bf16[1,1,96,384]{3,2,1,0:T(8,128)(2,1)S(1)}, bf16[1,1,96,384]{3,2,1,0:T(8,128)(2,1)S(1)}, u32[]{:S(2)}, u32[]{:S(2)}) collective-permute-start(bf16[1,1,96,384]{3,2,1,0:T(8,128)(2,1)S(1)} %get-tuple-element.122), channel_id=1, source_target_pairs={{1,0},{2,1},{3,2},{4,3},{5,4},{6,5},{7,6},{9,8},{10,9},{11,10},{12... | collective-permute-start | bytes 221192 | tf_op jit(solution)/shard_map/ppermute | solution.py:48
  200.3 30.4 %copy-start.35 = (f32[384]{0:T(512)S(1)}, f32[384]{0:T(512)}, u32[]{:S(2)}) copy-start(f32[384]{0:T(512)} %get-tuple-element.29) | copy-start | bytes 4612
  200.3 30.4 %copy-start.36 = (f32[384]{0:T(512)S(1)}, f32[384]{0:T(512)}, u32[]{:S(2)}) copy-start(f32[384]{0:T(512)} %get-tuple-element.194) | copy-start | bytes 4612
  220.8 9.9 %all-to-all-start.9 = ((f32[16,1,768]{2,1,0:T(1,128)}), f32[16,1,768]{2,1,0:T(1,128)S(1)}, u32[]{:S(2)}, u32[]{:S(2)}) async-start(f32[16,1,768]{2,1,0:T(1,128)} %broadcast_in_dim.75), calls=%async_computation.9 | async-start | bytes 98304 | tf_op jit(solution)/shard_map/all_to_all | solution.py:19
  242.4 4.7 %collective-permute-start.12 = (bf16[1,1,192,384]{3,2,1,0:T(8,128)(2,1)S(1)}, bf16[1,1,192,384]{3,2,1,0:T(8,128)(2,1)S(1)}, u32[]{:S(2)}, u32[]{:S(2)}) collective-permute-start(bf16[1,1,192,384]{3,2,1,0:T(8,128)(2,1)S(1)} %get-tuple-element.115), channel_id=1, source_target_pairs={{0,1},{1,2},{2,3},{3,4},{4,5},{5,6},{6,7},{8,9},{9,10},{10,11},{11... | collective-permute-start | bytes 442376 | tf_op jit(solution)/shard_map/ppermute | solution.py:45
  245.0 5.9 %collective-permute-start.13 = (bf16[1,1,192,384]{3,2,1,0:T(8,128)(2,1)S(1)}, bf16[1,1,192,384]{3,2,1,0:T(8,128)(2,1)S(1)}, u32[]{:S(2)}, u32[]{:S(2)}) collective-permute-start(bf16[1,1,192,384]{3,2,1,0:T(8,128)(2,1)S(1)} %get-tuple-element.116), channel_id=1, source_target_pairs={{1,0},{2,1},{3,2},{4,3},{5,4},{6,5},{7,6},{9,8},{10,9},{11,10},{12... | collective-permute-start | bytes 442376 | tf_op jit(solution)/shard_map/ppermute | solution.py:48
  253.8 27.2 %copy-start.41 = (f32[384]{0:T(512)S(1)}, f32[384]{0:T(512)}, u32[]{:S(2)}) copy-start(f32[384]{0:T(512)} %get-tuple-element.28) | copy-start | bytes 4612
  257.0 27.3 %copy-start.8 = (bf16[1,1,3,3,384]{4,1,3,2,0:T(2,128)(2,1)S(1)}, bf16[1,1,3,3,384]{4,1,3,2,0:T(2,128)(2,1)}, u32[]{:S(2)}) copy-start(bf16[1,1,3,3,384]{4,1,3,2,0:T(2,128)(2,1)} %get-tuple-element.131) | copy-start | bytes 20740
  257.0 27.3 %copy-start.9 = (bf16[1,1,3,3,384]{4,1,3,2,0:T(2,128)(2,1)S(1)}, bf16[1,1,3,3,384]{4,1,3,2,0:T(2,128)(2,1)}, u32[]{:S(2)}) copy-start(bf16[1,1,3,3,384]{4,1,3,2,0:T(2,128)(2,1)} %get-tuple-element.138) | copy-start | bytes 20740
  271.0 9.9 %all-to-all-start.11 = ((f32[16,1,768]{2,1,0:T(1,128)}), f32[16,1,768]{2,1,0:T(1,128)S(1)}, u32[]{:S(2)}, u32[]{:S(2)}) async-start(f32[16,1,768]{2,1,0:T(1,128)} %broadcast_in_dim.79), calls=%async_computation.11 | async-start | bytes 98304 | tf_op jit(solution)/shard_map/all_to_all | solution.py:19
  283.1 5.9 %collective-permute-start.14 = (bf16[1,1,192,384]{3,2,1,0:T(8,128)(2,1)S(1)}, bf16[1,1,192,384]{3,2,1,0:T(8,128)(2,1)S(1)}, u32[]{:S(2)}, u32[]{:S(2)}) collective-permute-start(bf16[1,1,192,384]{3,2,1,0:T(8,128)(2,1)S(1)} %slice.1108), channel_id=1, source_target_pairs={{1,0},{2,1},{3,2},{4,3},{5,4},{6,5},{7,6},{9,8},{10,9},{11,10},{12... | collective-permute-start | bytes 442376 | tf_op jit(solution)/shard_map/ppermute | solution.py:14
  293.8 4.9 %collective-permute-start.15 = (bf16[1,1,96,384]{3,2,1,0:T(8,128)(2,1)S(1)}, bf16[1,1,96,384]{3,2,1,0:T(8,128)(2,1)S(1)}, u32[]{:S(2)}, u32[]{:S(2)}) collective-permute-start(bf16[1,1,96,384]{3,2,1,0:T(8,128)(2,1)S(1)} %get-tuple-element.119), channel_id=1, source_target_pairs={{0,1},{1,2},{2,3},{3,4},{4,5},{5,6},{6,7},{8,9},{9,10},{10,11},{11... | collective-permute-start | bytes 221192 | tf_op jit(solution)/shard_map/ppermute | solution.py:45
  296.4 5.1 %collective-permute-start.16 = (bf16[1,1,96,384]{3,2,1,0:T(8,128)(2,1)S(1)}, bf16[1,1,96,384]{3,2,1,0:T(8,128)(2,1)S(1)}, u32[]{:S(2)}, u32[]{:S(2)}) collective-permute-start(bf16[1,1,96,384]{3,2,1,0:T(8,128)(2,1)S(1)} %get-tuple-element.120), channel_id=1, source_target_pairs={{1,0},{2,1},{3,2},{4,3},{5,4},{6,5},{7,6},{9,8},{10,9},{11,10},{12... | collective-permute-start | bytes 221192 | tf_op jit(solution)/shard_map/ppermute | solution.py:48
  298.6 29.4 %copy-start.45 = (f32[384]{0:T(512)S(1)}, f32[384]{0:T(512)}, u32[]{:S(2)}) copy-start(f32[384]{0:T(512)} %get-tuple-element.34) | copy-start | bytes 4612
  298.6 29.4 %copy-start.46 = (f32[384]{0:T(512)S(1)}, f32[384]{0:T(512)}, u32[]{:S(2)}) copy-start(f32[384]{0:T(512)} %get-tuple-element.189) | copy-start | bytes 4612
  302.1 31.5 %copy-start.25 = (f32[384]{0:T(512)S(1)}, f32[384]{0:T(512)}, u32[]{:S(2)}) copy-start(f32[384]{0:T(512)} %get-tuple-element.30) | copy-start | bytes 4612
  302.1 31.5 %copy-start.26 = (f32[384]{0:T(512)S(1)}, f32[384]{0:T(512)}, u32[]{:S(2)}) copy-start(f32[384]{0:T(512)} %get-tuple-element.193) | copy-start | bytes 4612
  302.1 31.5 %copy-start.30 = (f32[384]{0:T(512)S(1)}, f32[384]{0:T(512)}, u32[]{:S(2)}) copy-start(f32[384]{0:T(512)} %copy-done.29) | copy-start | bytes 4612
  302.1 31.5 %copy-start.32 = (f32[384]{0:T(512)S(1)}, f32[384]{0:T(512)}, u32[]{:S(2)}) copy-start(f32[384]{0:T(512)} %copy-done.31) | copy-start | bytes 4612
  328.0 40.5 %copy-start.43 = (f32[384]{0:T(512)S(1)}, f32[384]{0:T(512)}, u32[]{:S(2)}) copy-start(f32[384]{0:T(512)} %get-tuple-element.27) | copy-start | bytes 4612
  328.0 40.5 %copy-start.44 = (f32[384]{0:T(512)S(1)}, f32[384]{0:T(512)}, u32[]{:S(2)}) copy-start(f32[384]{0:T(512)} %get-tuple-element.196) | copy-start | bytes 4612
  328.2 41.1 %copy-start.2 = (bf16[1,4,96,384]{3,2,1,0:T(8,128)(2,1)}, bf16[1,4,96,384]{3,2,1,0:T(8,128)(2,1)S(1)}, u32[]{:S(2)}) copy-start(bf16[1,4,96,384]{3,2,1,0:T(8,128)(2,1)S(1)} %add_convert_fusion.4) | copy-start | bytes 884740
  328.2 5.1 %collective-permute-start.17 = (bf16[1,1,96,384]{3,2,1,0:T(8,128)(2,1)S(1)}, bf16[1,1,96,384]{3,2,1,0:T(8,128)(2,1)S(1)}, u32[]{:S(2)}, u32[]{:S(2)}) collective-permute-start(bf16[1,1,96,384]{3,2,1,0:T(8,128)(2,1)S(1)} %slice.1126), channel_id=1, source_target_pairs={{1,0},{2,1},{3,2},{4,3},{5,4},{6,5},{7,6},{9,8},{10,9},{11,10},{12... | collective-permute-start | bytes 221192 | tf_op jit(solution)/shard_map/ppermute | solution.py:14
  335.0 4.0 %collective-permute-start.18 = (bf16[1,1,48,384]{3,2,1,0:T(8,128)(2,1)S(1)}, bf16[1,1,48,384]{3,2,1,0:T(8,128)(2,1)S(1)}, u32[]{:S(2)}, u32[]{:S(2)}) collective-permute-start(bf16[1,1,48,384]{3,2,1,0:T(8,128)(2,1)S(1)} %get-tuple-element.127), channel_id=1, source_target_pairs={{0,1},{1,2},{2,3},{3,4},{4,5},{5,6},{6,7},{8,9},{9,10},{10,11},{11... | collective-permute-start | bytes 110600 | tf_op jit(solution)/shard_map/ppermute | solution.py:45
  337.7 4.7 %collective-permute-start.19 = (bf16[1,1,48,384]{3,2,1,0:T(8,128)(2,1)S(1)}, bf16[1,1,48,384]{3,2,1,0:T(8,128)(2,1)S(1)}, u32[]{:S(2)}, u32[]{:S(2)}) collective-permute-start(bf16[1,1,48,384]{3,2,1,0:T(8,128)(2,1)S(1)} %get-tuple-element.128), channel_id=1, source_target_pairs={{1,0},{2,1},{3,2},{4,3},{5,4},{6,5},{7,6},{9,8},{10,9},{11,10},{12... | collective-permute-start | bytes 110600 | tf_op jit(solution)/shard_map/ppermute | solution.py:48
  (24 other events, 186.8 us)
where the time goes:
time: 372 us; the launch traced here: 369 us
  blocking collectives  146 us (39%)
  waiting for transfers between devices  68.5 us (18%)
  starting transfers between devices  59.5 us (16%)
  other arithmetic  47.8 us (13%)
  local copies, waits for them, and re-layouts  26.8 us (7%)
  matrix products  13.7 us (4%)
  between operations  7.17 us (2%)
    all_to_all x11, blocking collectives, sent_to_all(): return lax.all_to_all(copies, axis, split_axis=0, concat_axis=0, tiled=True)  146 us
    all_to_all x5, waiting for transfers between devices, sent_to_all(): return lax.all_to_all(copies, axis, split_axis=0, concat_axis=0, tiled=True)  28.1 us
    ppermute x8, waiting for transfers between devices, extended_2(): lax.ppermute(lax.slice_in_dim(block, 0, width, axis=dim), axis, backward)  27.6 us
    ppermute x8, starting transfers between devices, extended_2(): lax.ppermute(lax.slice_in_dim(block, block.shape[dim] - width, None, axis...  22.9 us
    all_to_all x5, starting transfers between devices, sent_to_all(): return lax.all_to_all(copies, axis, split_axis=0, concat_axis=0, tiled=True)  20.8 us
    convert_element_type x8, other arithmetic, weighted_join_activate(): return jax.nn.silu(running / weight_sum).astype(jnp.bfloat16)  17 us
    dot_general x8, matrix products, separable(): jnp.dot(spatial.reshape(-1, spatial.shape[-1]), projection, preferred_ele...  13.7 us
    ppermute x4, waiting for transfers between devices, from_behind(): return lax.ppermute(block, axis, route)  11.6 us
  transfers between devices with their start and end apart: 25, of which 19 were waited for; matrix products, arithmetic and copies ran while one was open for 2% of the time, Pallas kernels for 0%

commit v1 on v0

v1 whole, which is shorter than its diff:
```python
import functools

import jax
import jax.numpy as jnp
from jax import lax
from jax.experimental import pallas as pl
from jax.experimental.pallas import tpu as pltpu
from jax.sharding import Mesh
from jax.sharding import PartitionSpec as P

LAYERS = 2
C = 384
T = 48
BATCH = ("batch_0", "batch_1", "batch_2")
FIRST = ("batch_0", "batch_1")
SECOND = ("batch_2", "rows")
F32 = jnp.float32
BF16 = jnp.bfloat16
LOW = -3.0e38


def vspec():
    return pl.BlockSpec(memory_space=pltpu.VMEM)


def sspec():
    return pl.BlockSpec(memory_space=pltpu.SMEM)


def from_left(plane):
    rolled = pltpu.roll(plane, 1, 0)
    at = lax.broadcasted_iota(jnp.int32, plane.shape, 0)
    return jnp.where(at == 0, 0.0, rolled)


def from_right(plane, fill=0.0):
    rolled = pltpu.roll(plane, plane.shape[0] - 1, 0)
    at = lax.broadcasted_iota(jnp.int32, plane.shape, 0)
    return jnp.where(at == plane.shape[0] - 1, fill, rolled)


def affine_of(totals_ref, gain, bias, count):
    totals = jnp.sum(totals_ref[...], axis=0)
    center = totals[:, :C] * (1.0 / count)
    spread = totals[:, C:] * (1.0 / count) - center * center
    scale = lax.rsqrt(spread + 1e-05) * gain
    return scale, bias - center * scale


def activate(half):
    return half + half * jnp.tanh(half)


def up32(x):
    return x.astype(F32)


def gain_bias(gain_ref, bias_ref, layer, n):
    return gain_ref[layer, n : n + 1, :], bias_ref[layer, n : n + 1, :]


def put_stats(stats_ref, total, square):
    line = jnp.concatenate([total, square], axis=1)
    for k in range(16):
        stats_ref[k] = line


def column_sum(x):
    return jnp.sum(x, axis=0, keepdims=True)


def conv_row(act_ref, taps, h, phases):
    out = []
    for f in range(phases):
        acc = None
        for j in (0, 2, 1):
            src, shift = f + j - 1, None
            if src < 0:
                src, shift = phases - 1, from_left
            elif src >= phases:
                src, shift = 0, from_right
            part = None
            for i in range(3):
                term = act_ref[h + i, src] * taps[i * 3 + j]
                part = term if part is None else part + term
            if shift is not None:
                part = shift(part)
            acc = part if acc is None else acc + part
        out.append(acc)
    return out


def load_taps(dw_ref, layer, n):
    return [up32(dw_ref[layer, n, i, j : j + 1, :]) for i in range(3) for j in range(3)]


def deinterleave(row, perm):
    return jnp.dot(perm, row, preferred_element_type=F32).astype(BF16)


def one_hot(width, phases, inverse=False):
    r = lax.broadcasted_iota(jnp.int32, (width, width), 0)
    c = lax.broadcasted_iota(jnp.int32, (width, width), 1)
    if inverse:
        r, c = c, r
    want = lax.rem(r, T) * phases + lax.div(r, T)
    return jnp.where(want == c, 1.0, 0.0).astype(BF16)


def prep_fine_kernel(x_ref, o_ref):
    perm = one_hot(4 * T, 4)

    def row(h, _):
        o_ref[h] = deinterleave(x_ref[0, h], perm).reshape(4, T, C)
        return 0

    lax.fori_loop(0, 8, row, 0)


def prep_mid_kernel(x_ref, up_ref, down_ref, o_ref):
    perm = one_hot(2 * T, 2)
    o_ref[0] = deinterleave(up_ref[: 2 * T, :], perm).reshape(2, T, C)
    for h in range(4):
        o_ref[h + 1] = deinterleave(x_ref[0, h], perm).reshape(2, T, C)
    o_ref[5] = deinterleave(down_ref[: 2 * T, :], perm).reshape(2, T, C)


def out_kernel(phases, rows, x_ref, aff_ref, o_ref):
    perm = one_hot(phases * T, phases, inverse=True)
    scale, shift = aff_ref[0:1, :], aff_ref[1:2, :]

    def row(h, _):
        planes = (up32(x_ref[h].reshape(phases * T, C)) * scale + shift).astype(BF16)
        o_ref[0, h] = jnp.dot(perm, planes, preferred_element_type=F32).astype(BF16)
        return 0

    lax.fori_loop(0, rows, row, 0)


def out_top_kernel(layer, count, x_ref, totals_ref, gain_ref, bias_ref, o_ref):
    scale, shift = affine_of(totals_ref, *gain_bias(gain_ref, bias_ref, layer, 3), count)
    for h in range(2):
        o_ref[0, h] = (up32(x_ref[h]) * scale + shift).astype(BF16)


def finish_small(act_ref, spatial_ref, p_ref, stats_ref, dw_ref, pw_ref, layer, n, rows, phases):
    taps = load_taps(dw_ref, layer, n)
    for h in range(rows):
        for f, plane in enumerate(conv_row(act_ref, taps, h, phases)):
            at = (h * phases + f) * T
            spatial_ref[at : at + T, :] = plane.astype(BF16)
    projected = jnp.dot(spatial_ref[...], pw_ref[layer, n], preferred_element_type=F32)
    put_stats(stats_ref, column_sum(projected), column_sum(projected * projected))
    p_ref[...] = projected.astype(BF16).reshape(p_ref.shape)


def k0_kernel(
    layer,
    count,
    flags_ref,
    w_ref,
    mid_above_ref,
    mid_ref,
    mid_below_ref,
    top_above_ref,
    top_ref,
    top_below_ref,
    mid_aff_ref,
    totals_ref,
    gain_ref,
    bias_ref,
    dw_ref,
    pw_ref,
    p_ref,
    stats_ref,
    aff_ref,
    act_ref,
    spatial_ref,
):
    w0, w1 = w_ref[layer * 6], w_ref[layer * 6 + 1]
    norm = 0.5 / (w0 + w1 + 0.0001)
    w0, w1 = w0 * norm, w1 * norm
    if layer:
        scale, shift = affine_of(totals_ref, *gain_bias(gain_ref, bias_ref, layer - 1, 3), count)
        aff_ref[0:1, :] = scale
        aff_ref[1:2, :] = shift
        a = mid_aff_ref[0:1, :] * w0
        b = scale * w1
        c = mid_aff_ref[1:2, :] * w0 + shift * w1
    else:
        aff_ref[...] = jnp.zeros(aff_ref.shape, F32)
        a, b, c = w0, w1, 0.0
    up_flag, down_flag = flags_ref[0], flags_ref[1]

    def top_row(i):
        if i < 0:
            return up32(top_above_ref[...])
        return up32(top_below_ref[...]) if i > 1 else up32(top_ref[i])

    for i in range(-1, 3):
        u = top_row(i) * b + c
        for r in (2 * i, 2 * i + 1):
            if r < -1 or r > 4:
                continue
            for p in range(2):
                if r < 0:
                    m = mid_above_ref[p]
                elif r > 3:
                    m = mid_below_ref[p]
                else:
                    m = mid_ref[r, p]
                act = activate(up32(m) * a + u)
                if r < 0:
                    act = act * up_flag
                elif r > 3:
                    act = act * down_flag
                act_ref[r + 1, p] = act
    finish_small(act_ref, spatial_ref, p_ref, stats_ref, dw_ref, pw_ref, layer, 0, 4, 2)


def k1_kernel(
    layer,
    count,
    flags_ref,
    w_ref,
    fine_above_ref,
    fine_ref,
    fine_below_ref,
    td_above_ref,
    td_ref,
    td_below_ref,
    fine_aff_ref,
    totals_ref,
    gain_ref,
    bias_ref,
    dw_ref,
    pw_ref,
    p_ref,
    stats_ref,
    aff_ref,
    u_ref,
    act_ref,
    spatial_ref,
):
    w0, w1 = w_ref[layer * 6 + 2], w_ref[layer * 6 + 3]
    norm = 0.5 / (w0 + w1 + 0.0001)
    w0, w1 = w0 * norm, w1 * norm
    scale, shift = affine_of(totals_ref, *gain_bias(gain_ref, bias_ref, layer, 0), count)
    aff_ref[0:1, :] = scale
    aff_ref[1:2, :] = shift
    b, c = scale * w1, shift * w1
    if layer:
        a = fine_aff_ref[0:1, :] * w0
        c = c + fine_aff_ref[1:2, :] * w0
    else:
        a = w0
    for p in range(2):
        u_ref[0, p] = up32(td_above_ref[p]) * b + c
        for i in range(4):
            u_ref[i + 1, p] = up32(td_ref[i, p]) * b + c
        u_ref[5, p] = up32(td_below_ref[p]) * b + c
    up_flag, down_flag = flags_ref[0], flags_ref[1]
    for f in range(4):
        act_ref[0, f] = activate(up32(fine_above_ref[f]) * a + u_ref[0, f // 2]) * up_flag
        act_ref[9, f] = activate(up32(fine_below_ref[f]) * a + u_ref[5, f // 2]) * down_flag

    def act_row(i, _):
        for q in range(2):
            for f in range(4):
                h = 2 * i + q
                act_ref[h + 1, f] = activate(up32(fine_ref[h, f]) * a + u_ref[i + 1, f // 2])
        return 0

    lax.fori_loop(0, 4, act_row, 0)
    taps = load_taps(dw_ref, layer, 1)

    def conv(h, carry):
        total, square = carry
        for f, plane in enumerate(conv_row(act_ref, taps, h, 4)):
            spatial_ref[f * T : (f + 1) * T, :] = plane.astype(BF16)
        projected = jnp.dot(spatial_ref[...], pw_ref[layer, 1], preferred_element_type=F32)
        p_ref[h] = projected.astype(BF16).reshape(4, T, C)
        return total + column_sum(projected), square + column_sum(projected * projected)

    zero = jnp.zeros((1, C), F32)
    total, square = lax.fori_loop(0, 8, conv, (zero, zero))
    put_stats(stats_ref, total, square)


def pool_fine_kernel(p_ref, up_ref, pool_ref):
    def column_pool(h):
        x = [up32(p_ref[h, f]) for f in range(4)]
        even = jnp.maximum(jnp.maximum(x[0], x[1]), x[2])
        odd = jnp.maximum(jnp.maximum(x[2], x[3]), from_right(x[0], LOW))
        return even, odd

    first = column_pool(0)
    upper = first
    for i in range(4):
        rows = [upper, column_pool(2 * i + 1)]
        if i < 3:
            upper = column_pool(2 * i + 2)
            rows.append(upper)
        for p in range(2):
            best = functools.reduce(jnp.maximum, [r[p] for r in rows]).astype(BF16)
            pool_ref[i, p] = best
            if i == 0:
                up_ref[0, p] = first[p].astype(BF16)
                up_ref[1, p] = best


def pool_mid_kernel(p_ref, up_ref, pool_ref):
    def column_pool(h):
        x = [up32(p_ref[h, f]) for f in range(2)]
        return jnp.maximum(jnp.maximum(x[0], x[1]), from_right(x[0], LOW))

    rows = [column_pool(h) for h in range(4)]
    best = jnp.maximum(jnp.maximum(rows[0], rows[1]), rows[2]).astype(BF16)
    pool_ref[0] = best
    pool_ref[1] = jnp.maximum(rows[2], rows[3]).astype(BF16)
    up_ref[0] = rows[0].astype(BF16)
    up_ref[1] = best


def k2_kernel(
    layer,
    count,
    flags_ref,
    w_ref,
    mid_above_ref,
    mid_ref,
    mid_below_ref,
    td_above_ref,
    td_ref,
    td_below_ref,
    pool_above_ref,
    pool_ref,
    pool_own_ref,
    pool_below_ref,
    mid_aff_ref,
    td_aff_ref,
    totals_ref,
    gain_ref,
    bias_ref,
    dw_ref,
    pw_ref,
    p_ref,
    stats_ref,
    aff_ref,
    act_ref,
    spatial_ref,
):
    w0, w1, w2 = (w_ref[12 + layer * 3 + k] for k in range(3))
    norm = 0.5 / (w0 + w1 + w2 + 0.0001)
    w0, w1, w2 = w0 * norm, w1 * norm, w2 * norm
    scale, shift = affine_of(totals_ref, *gain_bias(gain_ref, bias_ref, layer, 1), count)
    aff_ref[0:1, :] = scale
    aff_ref[1:2, :] = shift
    b = td_aff_ref[0:1, :] * w1
    d = scale * w2
    c = td_aff_ref[1:2, :] * w1 + shift * w2
    if layer:
        a = mid_aff_ref[0:1, :] * w0
        c = c + mid_aff_ref[1:2, :] * w0
    else:
        a = w0
    up_flag, down_flag = flags_ref[0], flags_ref[1]
    for r in range(-1, 5):
        for p in range(2):
            if r < 0:
                m, td = mid_above_ref[p], td_above_ref[p]
                pool = jnp.maximum(up32(pool_above_ref[p]), up32(pool_own_ref[0, p]))
            elif r > 3:
                m, td = mid_below_ref[p], td_below_ref[p]
                pool = up32(pool_below_ref[1, p])
            else:
                m, td = mid_ref[r, p], td_ref[r, p]
                pool = up32(pool_ref[r, p])
                if r == 3:
                    below = jnp.where(down_flag > 0.5, up32(pool_below_ref[0, p]), LOW)
                    pool = jnp.maximum(pool, below)
            act = activate(up32(m) * a + up32(td) * b + (pool * d + c))
            if r < 0:
                act = act * up_flag
            elif r > 3:
                act = act * down_flag
            act_ref[r + 1, p] = act
    finish_small(act_ref, spatial_ref, p_ref, stats_ref, dw_ref, pw_ref, layer, 2, 4, 2)


def k3_kernel(
    layer,
    count,
    flags_ref,
    w_ref,
    top_above_ref,
    top_ref,
    top_below_ref,
    pool_above_ref,
    pool_ref,
    pool_own_ref,
    pool_below_ref,
    top_aff_ref,
    totals_ref,
    gain_ref,
    bias_ref,
    dw_ref,
    pw_ref,
    p_ref,
    stats_ref,
    aff_ref,
    act_ref,
    spatial_ref,
):
    w0, w1 = w_ref[layer * 6 + 4], w_ref[layer * 6 + 5]
    norm = 0.5 / (w0 + w1 + 0.0001)
    w0, w1 = w0 * norm, w1 * norm
    scale, shift = affine_of(totals_ref, *gain_bias(gain_ref, bias_ref, layer, 2), count)
    aff_ref[0:1, :] = scale
    aff_ref[1:2, :] = shift
    d, c = scale * w1, shift * w1
    if layer:
        a = top_aff_ref[0:1, :] * w0
        c = c + top_aff_ref[1:2, :] * w0
    else:
        a = w0
    up_flag, down_flag = flags_ref[0], flags_ref[1]
    for r in range(-1, 3):
        if r < 0:
            m = top_above_ref[...]
            pool = jnp.maximum(up32(pool_above_ref[...]), up32(pool_own_ref[0]))
        elif r > 1:
            m = top_below_ref[...]
            pool = up32(pool_below_ref[1])
        else:
            m = top_ref[r]
            pool = up32(pool_ref[r])
            if r == 1:
                below = jnp.where(down_flag > 0.5, up32(pool_below_ref[0]), LOW)
                pool = jnp.maximum(pool, below)
        act = activate(up32(m) * a + (pool * d + c))
        if r < 0:
            act = act * up_flag
        elif r > 1:
            act = act * down_flag
        act_ref[r + 1, 0] = act
    finish_small(act_ref, spatial_ref, p_ref, stats_ref, dw_ref, pw_ref, layer, 3, 2, 1)


def call(kernel, outs, args, scalars=0, scratch=(), flops=1_000_000, name=None):
    single = isinstance(outs, tuple)
    shapes = [outs] if single else list(outs)
    result = pl.pallas_call(
        kernel,
        out_shape=[jax.ShapeDtypeStruct(s, d) for s, d in shapes],
        in_specs=[sspec()] * scalars + [vspec()] * (len(args) - scalars),
        out_specs=[vspec()] * len(shapes),
        scratch_shapes=list(scratch),
        compiler_params=pltpu.CompilerParams(vmem_limit_bytes=24 * 1024 * 1024),
        cost_estimate=pl.CostEstimate(flops=flops, bytes_accessed=1_000_000, transcendentals=0),
        name=name,
    )(*args)
    return result[0] if single else result


STATS = ((16, 1, 2 * C), F32)
AFF = ((2, C), F32)


def exchange(stats, axis):
    return lax.all_to_all(stats, axis, split_axis=0, concat_axis=0, tiled=True)


def reduce_stats(stats):
    near = exchange(stats, FIRST).sum(axis=0, keepdims=True)
    return exchange(jnp.broadcast_to(near, stats.shape), SECOND)


def send_down(x):
    n = lax.axis_size("rows")
    return lax.ppermute(x, "rows", [(i, i + 1) for i in range(n - 1)])


def send_up(x):
    n = lax.axis_size("rows")
    return lax.ppermute(x, "rows", [(i + 1, i) for i in range(n - 1)])


def small_scratch(rows, phases):
    return (
        pltpu.VMEM((rows + 2, phases, T, C), F32),
        pltpu.VMEM((rows * phases * T, C), BF16),
    )


def body(fine_in, mid_in, top_in, two, three, dw, pw, gain, bias):
    devices = lax.axis_size(BATCH) * lax.axis_size("rows")
    fine_count, mid_count, top_count = (float(k * T * devices) for k in (32, 8, 2))
    row = lax.axis_index("rows")
    flags = jnp.stack([row > 0, row < lax.axis_size("rows") - 1]).astype(F32)
    weights = jnp.concatenate([two.reshape(-1), three.reshape(-1)])
    no_aff = jnp.zeros((2, C), F32)
    no_totals = jnp.zeros((16, 1, 2 * C), F32)

    from_above = send_down(jnp.concatenate([mid_in[0, 3], top_in[0, 1]], axis=0))
    from_below = send_up(jnp.concatenate([mid_in[0, 0], top_in[0, 0]], axis=0))
    fine = call(prep_fine_kernel, ((8, 4, T, C), BF16), [fine_in], flops=6_000_000, name="prep_fine")
    mid_all = call(
        prep_mid_kernel, ((6, 2, T, C), BF16), [mid_in, from_above, from_below], name="prep_mid"
    )
    mid = (mid_all[0], mid_all[1:5], mid_all[5])
    top = (from_above[2 * T :], top_in[0], from_below[2 * T :])
    mid_aff, top_aff, fine_aff = no_aff, no_aff, no_aff
    top_totals = no_totals
    params = [gain, bias, dw, pw]
    fine_halo = None

    for layer in range(LAYERS):
        last = layer == LAYERS - 1
        p0, stats, new_top_aff = call(
            functools.partial(k0_kernel, layer, top_count),
            [((4, 2, T, C), BF16), STATS, AFF],
            [flags, weights, *mid, *top, mid_aff, top_totals, *params],
            scalars=2,
            scratch=small_scratch(4, 2),
            name=f"node0_{layer}",
        )
        top_aff = new_top_aff
        td = (send_down(p0[3]), p0, send_up(p0[0]))
        if fine_halo is None:
            fine_halo = (send_down(fine[7]), send_up(fine[0]))
        totals = reduce_stats(stats)

        p1, stats, td_aff = call(
            functools.partial(k1_kernel, layer, mid_count),
            [((8, 4, T, C), BF16), STATS, AFF],
            [flags, weights, fine_halo[0], fine, fine_halo[1], *td, fine_aff, totals, *params],
            scalars=2,
            scratch=(
                pltpu.VMEM((6, 2, T, C), F32),
                pltpu.VMEM((10, 4, T, C), F32),
                pltpu.VMEM((4 * T, C), BF16),
            ),
            flops=4_000_000,
            name=f"node1_{layer}",
        )
        pool_up, pool = call(
            pool_fine_kernel,
            [((2, 2, T, C), BF16), ((4, 2, T, C), BF16)],
            [p1],
            flops=2_000_000,
            name=f"pool_fine_{layer}",
        )
        pool_args = (send_down(pool[3]), pool, pool_up, send_up(pool_up))
        totals = reduce_stats(stats)

        p2, stats, fine_aff = call(
            functools.partial(k2_kernel, layer, fine_count),
            [((4, 2, T, C), BF16), STATS, AFF],
            [flags, weights, *mid, *td, *pool_args, mid_aff, td_aff, totals, *params],
            scalars=2,
            scratch=small_scratch(4, 2),
            name=f"node2_{layer}",
        )
        pool_up, pool = call(
            pool_mid_kernel,
            [((2, T, C), BF16), ((2, T, C), BF16)],
            [p2],
            name=f"pool_mid_{layer}",
        )
        pool_args = (send_down(pool[1]), pool, pool_up, send_up(pool_up))
        if last:
            fine_out = call(
                functools.partial(out_kernel, 4, 8),
                ((1, 8, 4 * T, C), BF16),
                [p1, fine_aff],
                flops=6_000_000,
                name="out_fine",
            )
        else:
            mid_next = (send_down(p2[3]), p2, send_up(p2[0]))
        totals = reduce_stats(stats)

        p3, stats, mid_aff = call(
            functools.partial(k3_kernel, layer, mid_count),
            [((2, T, C), BF16), STATS, AFF],
            [flags, weights, *top, *pool_args, top_aff, totals, *params],
            scalars=2,
            scratch=small_scratch(2, 1),
            name=f"node3_{layer}",
        )
        if last:
            mid_out = call(
                functools.partial(out_kernel, 2, 4),
                ((1, 4, 2 * T, C), BF16),
                [p2, mid_aff],
                flops=2_000_000,
                name="out_mid",
            )
        else:
            top = (send_down(p3[1]), p3, send_up(p3[0]))
            mid = mid_next
            fine = p1
            fine_halo = (send_down(p1[7]), send_up(p1[0]))
        top_totals = reduce_stats(stats)

    top_out = call(
        functools.partial(out_top_kernel, LAYERS - 1, top_count),
        ((1, 2, T, C), BF16),
        [p3, top_totals, gain, bias],
        name="out_top",
    )
    return fine_out, mid_out, top_out


def solution(mesh):
    split = Mesh(
        mesh.devices.reshape(4, 4, 2, mesh.shape["rows"]), ("batch_0", "batch_1", "batch_2", "rows")
    )
    level = P(BATCH, "rows", None, None)
    in_specs = (level,) * 3 + (P(),) * 6
    return jax.shard_map(
        body, mesh=split, in_specs=in_specs, out_specs=(level,) * 3, check_vma=False
    )
```

time: 372 us -> 355 us (0.954)
  blocking collectives: 146 us -> 9.3 us
  starting transfers between devices: 59.5 us -> 179 us
  local copies, waits for them, and re-layouts: 26.8 us -> 93.4 us
  other arithmetic: 47.8 us -> 7.58 us
  waiting for transfers between devices: 68.5 us -> 30 us
  Pallas kernels: 0 us -> 28.5 us
  matrix products: 13.7 us -> 0 us
  between operations: 7.17 us -> 1.49 us
    all_to_all x11 -> x1, blocking collectives: 146 us -> 9.3 us  [exchange(): return lax.all_to_all(stats, axis, split_axis=0, concat_axis=0, tiled=True)]
    all_to_all x5 -> x15, starting transfers between devices: 20.8 us -> 121 us  [exchange(): return lax.all_to_all(stats, axis, split_axis=0, concat_axis=0, tiled=True)]
    unnamed x98 -> x236, local copies, waits for them, and re-layouts: 2.01 us -> 74 us
    ppermute x20 -> x22, waiting for transfers between devices: 40.4 us -> 6.09 us  [the longest x11 5.7 us: send_down(): return lax.ppermute(x, 'rows', [(i, i + 1) for i in range(n - 1)])]
    convert_element_type x29 -> x1, other arithmetic: 29.2 us -> 0.08 us  [body(): flags = jnp.stack([row > 0, row < lax.axis_size('rows') - 1]).astype(F32)]
    pallas_call x0 -> x17, Pallas kernels: none -> 28.5 us  [call(): pl.pallas_call(kernel, out_shape=[jax.ShapeDtypeStruct(s, d) for s, d in...]
    ppermute x20 -> x22, starting transfers between devices: 38.8 us -> 58.3 us  [the longest x11 44.2 us: send_down(): return lax.ppermute(x, 'rows', [(i, i + 1) for i in range(n - 1)])]
    dot_general x8 -> x0, matrix products: 13.7 us -> none  [separable(): jnp.dot(spatial.reshape(-1, spatial.shape[-1]), projection, preferred_ele...]
  transfers between devices with their start and end apart: 25 -> 37, of which waited for: 19 -> 16; matrix products, arithmetic and copies ran while one was open for 2% -> 7% of each run, Pallas kernels for 0% -> 2%
where the time goes in v1:
time: 355 us; the launch traced here: 350 us
  starting transfers between devices  179 us (50%)
  local copies, waits for them, and re-layouts  93.4 us (26%)
  waiting for transfers between devices  30 us (8%)
  Pallas kernels  28.5 us (8%)
  blocking collectives  9.3 us (3%)
  other arithmetic  7.58 us (2%)
    all_to_all x15, starting transfers between devices, exchange(): return lax.all_to_all(stats, axis, split_axis=0, concat_axis=0, tiled=True)  121 us
    unnamed x236, local copies, waits for them, and re-layouts  74 us
    ppermute x11, starting transfers between devices, send_down(): return lax.ppermute(x, 'rows', [(i, i + 1) for i in range(n - 1)])  44.2 us
    pallas_call x17, Pallas kernels, call(): pl.pallas_call(kernel, out_shape=[jax.ShapeDtypeStruct(s, d) for s, d in...  28.5 us
    all_to_all x15, waiting for transfers between devices, exchange(): return lax.all_to_all(stats, axis, split_axis=0, concat_axis=0, tiled=True)  23.9 us
    ppermute x11, starting transfers between devices, send_up(): return lax.ppermute(x, 'rows', [(i + 1, i) for i in range(n - 1)])  14.1 us
    all_to_all x1, blocking collectives, exchange(): return lax.all_to_all(stats, axis, split_axis=0, concat_axis=0, tiled=True)  9.3 us
    broadcast_in_dim x8, local copies, waits for them, and re-layouts, reduce_stats(): return exchange(jnp.broadcast_to(near, stats.shape), SECOND)  7.16 us
  transfers between devices with their start and end apart: 37, of which 16 were waited for; matrix products, arithmetic and copies ran while one was open for 7% of the time, Pallas kernels for 2%

profile of v1, /device:TPU:1, one launch (start us, length us, event | category | flops | bytes accessed | tf_op | source)
XLA Modules:
  0.0 349.6 jit_solution(10038786458874475950)
XLA Ops:
  3.0 5.0 %collective-permute-start.2 = (bf16[144,384]{1,0:T(8,128)(2,1)}, bf16[144,384]{1,0:T(8,128)(2,1)}, u32[]{:S(2)}, u32[]{:S(2)}) collective-permute-start(bf16[144,384]{1,0:T(8,128)(2,1)} %pad_maximum_fusion), channel_id=1, source_target_pairs={{0,1},{1,2},{2,3},{3,4},{4,5},{5,6},{6,7},{8,9},{9,10},{10,11},{11... | collective-permute-start | bytes 331784 | tf_op jit(solution)/shard_map/ppermute | solution.py:481
  14.2 1.7 prep_fine.1.fine_ref
  20.4 1.4 node0_0.1
  23.8 6.8 %all-to-all-start = ((f32[16,1,768]{2,1,0:T(1,128)}), f32[16,1,768]{2,1,0:T(1,128)}, u32[]{:S(2)}, u32[]{:S(2)}) async-start(f32[16,1,768]{2,1,0:T(1,128)} %copy-done.83), calls=%async_computation | async-start | bytes 98304 | tf_op jit(solution)/shard_map/all_to_all | solution.py:471
  32.6 4.6 %collective-permute-start = (bf16[4,48,384]{2,1,0:T(8,128)(2,1)}, bf16[4,48,384]{2,1,0:T(8,128)(2,1)S(1)}, u32[]{:S(2)}, u32[]{:S(2)}) collective-permute-start(bf16[4,48,384]{2,1,0:T(8,128)(2,1)} %get-tuple-element.70), channel_id=1, source_target_pairs={{0,1},{1,2},{2,3},{3,4},{4,5},{5,6},{6,7},{8,9},{9,10},{10,11},{11... | collective-permute-start | bytes 442376 | tf_op jit(solution)/shard_map/ppermute | solution.py:481
  38.8 12.0 %all-to-all-start.1 = ((f32[16,1,768]{2,1,0:T(1,128)}), f32[16,1,768]{2,1,0:T(1,128)S(1)}, u32[]{:S(2)}, u32[]{:S(2)}) async-start(f32[16,1,768]{2,1,0:T(1,128)} %broadcast_in_dim.22), calls=%async_computation.1 | async-start | bytes 98304 | tf_op jit(solution)/shard_map/all_to_all | solution.py:471
  53.0 4.0 %collective-permute-start.4 = (bf16[2,48,384]{2,1,0:T(8,128)(2,1)S(1)}, bf16[2,48,384]{2,1,0:T(8,128)(2,1)S(1)}, u32[]{:S(2)}, u32[]{:S(2)}) collective-permute-start(bf16[2,48,384]{2,1,0:T(8,128)(2,1)S(1)} %get-tuple-element.78), channel_id=1, source_target_pairs={{0,1},{1,2},{2,3},{3,4},{4,5},{5,6},{6,7},{8,9},{9,10},{10,11},{11... | collective-permute-start | bytes 221192 | tf_op jit(solution)/shard_map/ppermute | solution.py:481
  69.7 4.4 %node1_0.1 = (bf16[8,4,48,384]{3,2,1,0:T(8,128)(2,1)S(1)}, f32[16,1,768]{2,1,0:T(1,128)S(1)}, f32[2,384]{1,0:T(2,128)S(1)}) custom-call(f32[2]{0:T(128)S(1)} %copy-done.90, f32[18]{0:T(128)S(1)} %copy-done.95, bf16[4,48,384]{2,1,0:T(8,128)(2,1)S(1)} %copy-done.69, bf16[8,4,48,384]{3,2,1,0:T(8,128)(2,1)S(1)} %copy-done.2, bf16[4,48,384]{2,1,0:T(8,128)(2,1)S(1)} %copy-done.67, ...), custom_call_target="tpu_custom_call" | custom-call | flops 4000000 | bytes 1000000 | tf_op jit(solution)/shard_map/node1_0/pallas_call | solution.py:453
  75.4 5.9 %all-to-all-start.2 = ((f32[16,1,768]{2,1,0:T(1,128)}), f32[16,1,768]{2,1,0:T(1,128)}, u32[]{:S(2)}, u32[]{:S(2)}) async-start(f32[16,1,768]{2,1,0:T(1,128)} %copy-done.86), calls=%async_computation.2 | async-start | bytes 98304 | tf_op jit(solution)/shard_map/all_to_all | solution.py:471
  84.0 3.8 %all-to-all-done.2 = f32[16,1,768]{2,1,0:T(1,128)} async-done(((f32[16,1,768]{2,1,0:T(1,128)}), f32[16,1,768]{2,1,0:T(1,128)}, u32[]{:S(2)}, u32[]{:S(2)}) %all-to-all-start.2) | async-done | bytes 49184 | tf_op jit(solution)/shard_map/all_to_all | solution.py:471
  87.8 1.4 reduce_sum.73
  90.6 11.3 %all-to-all-start.3 = ((f32[16,1,768]{2,1,0:T(1,128)}), f32[16,1,768]{2,1,0:T(1,128)}, u32[]{:S(2)}, u32[]{:S(2)}) async-start(f32[16,1,768]{2,1,0:T(1,128)} %broadcast_in_dim.23), calls=%async_computation.3 | async-start | bytes 98304 | tf_op jit(solution)/shard_map/all_to_all | solution.py:471
  102.8 3.2 collective-permute-start.8
  120.0 2.0 node2_0.1
  123.9 4.1 %all-to-all-start.4 = ((f32[16,1,768]{2,1,0:T(1,128)}), f32[16,1,768]{2,1,0:T(1,128)}, u32[]{:S(2)}, u32[]{:S(2)}) async-start(f32[16,1,768]{2,1,0:T(1,128)} %copy-done.80), calls=%async_computation.4 | async-start | bytes 98304 | tf_op jit(solution)/shard_map/all_to_all | solution.py:471
  131.7 2.9 all-to-all-done.4
  136.0 10.1 %all-to-all-start.5 = ((f32[16,1,768]{2,1,0:T(1,128)}), f32[16,1,768]{2,1,0:T(1,128)}, u32[]{:S(2)}, u32[]{:S(2)}) async-start(f32[16,1,768]{2,1,0:T(1,128)} %broadcast_in_dim.24), calls=%async_computation.5 | async-start | bytes 98304 | tf_op jit(solution)/shard_map/all_to_all | solution.py:471
  146.9 3.2 collective-permute-start.12
  151.9 1.5 all-to-all-done.5.totals_ref
  164.3 4.1 %all-to-all-start.6 = ((f32[16,1,768]{2,1,0:T(1,128)}), f32[16,1,768]{2,1,0:T(1,128)}, u32[]{:S(2)}, u32[]{:S(2)}) async-start(f32[16,1,768]{2,1,0:T(1,128)} %copy-done.81), calls=%async_computation.6 | async-start | bytes 98304 | tf_op jit(solution)/shard_map/all_to_all | solution.py:471
  168.4 1.6 slice_bitcast_fusion.9
  171.3 4.6 %collective-permute-start.10 = (bf16[2,48,384]{2,1,0:T(8,128)(2,1)}, bf16[2,48,384]{2,1,0:T(8,128)(2,1)}, u32[]{:S(2)}, u32[]{:S(2)}) collective-permute-start(bf16[2,48,384]{2,1,0:T(8,128)(2,1)} %get-tuple-element.76), channel_id=1, source_target_pairs={{0,1},{1,2},{2,3},{3,4},{4,5},{5,6},{6,7},{8,9},{9,10},{10,11},{11... | collective-permute-start | bytes 221192 | tf_op jit(solution)/shard_map/ppermute | solution.py:481
  175.9 1.4 reduce_sum.75
  178.7 8.8 %all-to-all-start.7 = ((f32[16,1,768]{2,1,0:T(1,128)}), f32[16,1,768]{2,1,0:T(1,128)}, u32[]{:S(2)}, u32[]{:S(2)}) async-start(f32[16,1,768]{2,1,0:T(1,128)} %broadcast_in_dim.25), calls=%async_computation.7 | async-start | bytes 98304 | tf_op jit(solution)/shard_map/all_to_all | solution.py:471
  189.6 4.0 %collective-permute-start.14 = (bf16[48,384]{1,0:T(8,128)(2,1)S(1)}, bf16[48,384]{1,0:T(8,128)(2,1)S(1)}, u32[]{:S(2)}, u32[]{:S(2)}) collective-permute-start(bf16[48,384]{1,0:T(8,128)(2,1)S(1)} %get-tuple-element.82), channel_id=1, source_target_pairs={{0,1},{1,2},{2,3},{3,4},{4,5},{5,6},{6,7},{8,9},{9,10},{10,11},{11... | collective-permute-start | bytes 110600 | tf_op jit(solution)/shard_map/ppermute | solution.py:481
  201.5 1.8 node0_1.1
  205.3 6.7 %all-to-all-start.8 = ((f32[16,1,768]{2,1,0:T(1,128)}), f32[16,1,768]{2,1,0:T(1,128)}, u32[]{:S(2)}, u32[]{:S(2)}) async-start(f32[16,1,768]{2,1,0:T(1,128)} %copy-done.84), calls=%async_computation.8 | async-start | bytes 98304 | tf_op jit(solution)/shard_map/all_to_all | solution.py:471
  214.0 5.0 %collective-permute-start.6 = (bf16[4,48,384]{2,1,0:T(8,128)(2,1)}, bf16[4,48,384]{2,1,0:T(8,128)(2,1)}, u32[]{:S(2)}, u32[]{:S(2)}) collective-permute-start(bf16[4,48,384]{2,1,0:T(8,128)(2,1)} %get-tuple-element.68), channel_id=1, source_target_pairs={{0,1},{1,2},{2,3},{3,4},{4,5},{5,6},{6,7},{8,9},{9,10},{10,11},{11... | collective-permute-start | bytes 442376 | tf_op jit(solution)/shard_map/ppermute | solution.py:481
  219.0 1.4 reduce_sum.76
  221.8 11.4 %all-to-all-start.9 = ((f32[16,1,768]{2,1,0:T(1,128)}), f32[16,1,768]{2,1,0:T(1,128)}, u32[]{:S(2)}, u32[]{:S(2)}) async-start(f32[16,1,768]{2,1,0:T(1,128)} %broadcast_in_dim.26), calls=%async_computation.9 | async-start | bytes 98304 | tf_op jit(solution)/shard_map/all_to_all | solution.py:471
  235.4 4.0 %collective-permute-start.16 = (bf16[2,48,384]{2,1,0:T(8,128)(2,1)S(1)}, bf16[2,48,384]{2,1,0:T(8,128)(2,1)S(1)}, u32[]{:S(2)}, u32[]{:S(2)}) collective-permute-start(bf16[2,48,384]{2,1,0:T(8,128)(2,1)S(1)} %get-tuple-element.74), channel_id=1, source_target_pairs={{0,1},{1,2},{2,3},{3,4},{4,5},{5,6},{6,7},{8,9},{9,10},{10,11},{11... | collective-permute-start | bytes 221192 | tf_op jit(solution)/shard_map/ppermute | solution.py:481
  247.1 4.8 %node1_1.1 = (bf16[8,4,48,384]{3,2,1,0:T(8,128)(2,1)S(1)}, f32[16,1,768]{2,1,0:T(1,128)S(1)}, f32[2,384]{1,0:T(2,128)S(1)}) custom-call(f32[2]{0:T(128)S(1)} %copy-done.93, f32[18]{0:T(128)S(1)} %copy-done.99, bf16[4,48,384]{2,1,0:T(8,128)(2,1)} %collective-permute-done.6.fine_above_ref, bf16[8,4,48,384]{3,2,1,0:T(8,128)(2,1)S(1)} %get-tuple-element.37.p_ref.fine_ref, ...), custom_call_target="tpu_custom_call" | custom-call | flops 4000000 | bytes 1000000 | tf_op jit(solution)/shard_map/node1_1/pallas_call | solution.py:453
  254.2 6.0 %all-to-all-start.10 = ((f32[16,1,768]{2,1,0:T(1,128)}), f32[16,1,768]{2,1,0:T(1,128)S(1)}, u32[]{:S(2)}, u32[]{:S(2)}) async-start(f32[16,1,768]{2,1,0:T(1,128)} %copy-done.85), calls=%async_computation.10 | async-start | bytes 98304 | tf_op jit(solution)/shard_map/all_to_all | solution.py:471
  263.0 3.6 %all-to-all-done.10 = f32[16,1,768]{2,1,0:T(1,128)S(1)} async-done(((f32[16,1,768]{2,1,0:T(1,128)}), f32[16,1,768]{2,1,0:T(1,128)S(1)}, u32[]{:S(2)}, u32[]{:S(2)}) %all-to-all-start.10) | async-done | bytes 49184 | tf_op jit(solution)/shard_map/all_to_all | solution.py:471
  267.3 11.9 %all-to-all-start.11 = ((f32[16,1,768]{2,1,0:T(1,128)}), f32[16,1,768]{2,1,0:T(1,128)S(1)}, u32[]{:S(2)}, u32[]{:S(2)}) async-start(f32[16,1,768]{2,1,0:T(1,128)} %broadcast_in_dim.27), calls=%async_computation.11 | async-start | bytes 98304 | tf_op jit(solution)/shard_map/all_to_all | solution.py:471
  279.2 3.3 collective-permute-start.18
  282.5 1.4 collective-permute-done.18.pool_above_ref
  284.5 1.7 all-to-all-done.11.totals_ref
  291.6 2.0 node2_1.1
  294.8 3.5 %all-to-all-start.12 = ((f32[16,1,768]{2,1,0:T(1,128)}), f32[16,1,768]{2,1,0:T(1,128)S(1)}, u32[]{:S(2)}, u32[]{:S(2)}) async-start(f32[16,1,768]{2,1,0:T(1,128)} %copy-done.82), calls=%async_computation.12 | async-start | bytes 98304 | tf_op jit(solution)/shard_map/all_to_all | solution.py:471
  299.7 5.0 %all-to-all-done.12 = f32[16,1,768]{2,1,0:T(1,128)S(1)} async-done(((f32[16,1,768]{2,1,0:T(1,128)}), f32[16,1,768]{2,1,0:T(1,128)S(1)}, u32[]{:S(2)}, u32[]{:S(2)}) %all-to-all-start.12) | async-done | bytes 49184 | tf_op jit(solution)/shard_map/all_to_all | solution.py:471
  305.4 9.6 %all-to-all-start.13 = ((f32[16,1,768]{2,1,0:T(1,128)}), f32[16,1,768]{2,1,0:T(1,128)S(1)}, u32[]{:S(2)}, u32[]{:S(2)}) async-start(f32[16,1,768]{2,1,0:T(1,128)} %broadcast_in_dim.28), calls=%async_computation.13 | async-start | bytes 98304 | tf_op jit(solution)/shard_map/all_to_all | solution.py:471
  315.1 3.3 collective-permute-start.20
  319.4 2.8 all-to-all-done.13.totals_ref
  323.2 9.3 %all_to_all.80 = f32[16,1,768]{2,1,0:T(1,128)S(1)} all-to-all(f32[16,1,768]{2,1,0:T(1,128)S(1)} %get-tuple-element.66), channel_id=1, replica_groups=mesh['batch_0'=4,'batch_1'=4,'batch_2'=2,'rows'=8] {'batch_0','batch_1'}, dimensions={0} | all-to-all | bytes 98304 | tf_op jit(solution)/shard_map/all_to_all | solution.py:471
  333.2 8.7 %all-to-all-start.15 = ((f32[16,1,768]{2,1,0:T(1,128)}), f32[16,1,768]{2,1,0:T(1,128)S(1)}, u32[]{:S(2)}, u32[]{:S(2)}) async-start(f32[16,1,768]{2,1,0:T(1,128)} %broadcast_in_dim.29), calls=%async_computation.15 | async-start | bytes 98304 | tf_op jit(solution)/shard_map/all_to_all | solution.py:471
  343.1 2.8 out_fine.1
  347.3 1.6 all-to-all-done.15.totals_ref
  (320 shorter events, 122.5 us)
Async XLA Ops:
  3.0 13.1 %collective-permute-start.2 = (bf16[144,384]{1,0:T(8,128)(2,1)}, bf16[144,384]{1,0:T(8,128)(2,1)}, u32[]{:S(2)}, u32[]{:S(2)}) collective-permute-start(bf16[144,384]{1,0:T(8,128)(2,1)} %pad_maximum_fusion), channel_id=1, source_target_pairs={{0,1},{1,2},{2,3},{3,4},{4,5},{5,6},{6,7},{8,9},{9,10},{10,11},{11... | collective-permute-start | bytes 331784 | tf_op jit(solution)/shard_map/ppermute | solution.py:481
  8.7 7.4 %collective-permute-start.3 = (bf16[144,384]{1,0:T(8,128)(2,1)}, bf16[144,384]{1,0:T(8,128)(2,1)}, u32[]{:S(2)}, u32[]{:S(2)}) collective-permute-start(bf16[144,384]{1,0:T(8,128)(2,1)} %pad_maximum_fusion.1), channel_id=1, source_target_pairs={{1,0},{2,1},{3,2},{4,3},{5,4},{6,5},{7,6},{9,8},{10,9},{11,10},{12... | collective-permute-start | bytes 331784 | tf_op jit(solution)/shard_map/ppermute | solution.py:486
  15.9 14.7 %copy-start.1 = (bf16[8,4,48,384]{3,2,1,0:T(8,128)(2,1)}, bf16[8,4,48,384]{3,2,1,0:T(8,128)(2,1)S(1)}, u32[]{:S(2)}) copy-start(bf16[8,4,48,384]{3,2,1,0:T(8,128)(2,1)S(1)} %prep_fine.1.fine_ref) | copy-start | bytes 3538948
  23.8 13.5 %all-to-all-start = ((f32[16,1,768]{2,1,0:T(1,128)}), f32[16,1,768]{2,1,0:T(1,128)}, u32[]{:S(2)}, u32[]{:S(2)}) async-start(f32[16,1,768]{2,1,0:T(1,128)} %copy-done.83), calls=%async_computation | async-start | bytes 98304 | tf_op jit(solution)/shard_map/all_to_all | solution.py:471
  31.4 25.6 %collective-permute-start.1 = (bf16[4,48,384]{2,1,0:T(8,128)(2,1)}, bf16[4,48,384]{2,1,0:T(8,128)(2,1)S(1)}, u32[]{:S(2)}, u32[]{:S(2)}) collective-permute-start(bf16[4,48,384]{2,1,0:T(8,128)(2,1)} %get-tuple-element.69), channel_id=1, source_target_pairs={{1,0},{2,1},{3,2},{4,3},{5,4},{6,5},{7,6},{9,8},{10,9},{11,10},{12... | collective-permute-start | bytes 442376 | tf_op jit(solution)/shard_map/ppermute | solution.py:486
  32.6 25.0 %collective-permute-start = (bf16[4,48,384]{2,1,0:T(8,128)(2,1)}, bf16[4,48,384]{2,1,0:T(8,128)(2,1)S(1)}, u32[]{:S(2)}, u32[]{:S(2)}) collective-permute-start(bf16[4,48,384]{2,1,0:T(8,128)(2,1)} %get-tuple-element.70), channel_id=1, source_target_pairs={{0,1},{1,2},{2,3},{3,4},{4,5},{5,6},{6,7},{8,9},{9,10},{10,11},{11... | collective-permute-start | bytes 442376 | tf_op jit(solution)/shard_map/ppermute | solution.py:481
  38.8 20.8 %all-to-all-start.1 = ((f32[16,1,768]{2,1,0:T(1,128)}), f32[16,1,768]{2,1,0:T(1,128)S(1)}, u32[]{:S(2)}, u32[]{:S(2)}) async-start(f32[16,1,768]{2,1,0:T(1,128)} %broadcast_in_dim.22), calls=%async_computation.1 | async-start | bytes 98304 | tf_op jit(solution)/shard_map/all_to_all | solution.py:471
  51.7 6.6 %collective-permute-start.5 = (bf16[2,48,384]{2,1,0:T(8,128)(2,1)S(1)}, bf16[2,48,384]{2,1,0:T(8,128)(2,1)S(1)}, u32[]{:S(2)}, u32[]{:S(2)}) collective-permute-start(bf16[2,48,384]{2,1,0:T(8,128)(2,1)S(1)} %get-tuple-element.77), channel_id=1, source_target_pairs={{1,0},{2,1},{3,2},{4,3},{5,4},{6,5},{7,6},{9,8},{10,9},{11,10},{12... | collective-permute-start | bytes 221192 | tf_op jit(solution)/shard_map/ppermute | solution.py:486
  53.0 6.0 %collective-permute-start.4 = (bf16[2,48,384]{2,1,0:T(8,128)(2,1)S(1)}, bf16[2,48,384]{2,1,0:T(8,128)(2,1)S(1)}, u32[]{:S(2)}, u32[]{:S(2)}) collective-permute-start(bf16[2,48,384]{2,1,0:T(8,128)(2,1)S(1)} %get-tuple-element.78), channel_id=1, source_target_pairs={{0,1},{1,2},{2,3},{3,4},{4,5},{5,6},{6,7},{8,9},{9,10},{10,11},{11... | collective-permute-start | bytes 221192 | tf_op jit(solution)/shard_map/ppermute | solution.py:481
  75.4 12.4 %all-to-all-start.2 = ((f32[16,1,768]{2,1,0:T(1,128)}), f32[16,1,768]{2,1,0:T(1,128)}, u32[]{:S(2)}, u32[]{:S(2)}) async-start(f32[16,1,768]{2,1,0:T(1,128)} %copy-done.86), calls=%async_computation.2 | async-start | bytes 98304 | tf_op jit(solution)/shard_map/all_to_all | solution.py:471
  82.8 26.3 %collective-permute-start.9 = (bf16[2,2,48,384]{3,2,1,0:T(8,128)(2,1)}, bf16[2,2,48,384]{3,2,1,0:T(8,128)(2,1)}, u32[]{:S(2)}, u32[]{:S(2)}) collective-permute-start(bf16[2,2,48,384]{3,2,1,0:T(8,128)(2,1)} %get-tuple-element.39.pool_own_ref), channel_id=1, source_target_pairs={{1,0},{2,1},{3,2},{4,3},{5,4},{6,5},{7,6},{9,8},{10,9},{11,10},{12... | collective-permute-start | bytes 442376 | tf_op jit(solution)/shard_map/ppermute | solution.py:486
  90.6 18.5 %all-to-all-start.3 = ((f32[16,1,768]{2,1,0:T(1,128)}), f32[16,1,768]{2,1,0:T(1,128)}, u32[]{:S(2)}, u32[]{:S(2)}) async-start(f32[16,1,768]{2,1,0:T(1,128)} %broadcast_in_dim.23), calls=%async_computation.3 | async-start | bytes 98304 | tf_op jit(solution)/shard_map/all_to_all | solution.py:471
  102.8 4.6 %collective-permute-start.8 = (bf16[2,48,384]{2,1,0:T(8,128)(2,1)S(1)}, bf16[2,48,384]{2,1,0:T(8,128)(2,1)S(1)}, u32[]{:S(2)}, u32[]{:S(2)}) collective-permute-start(bf16[2,48,384]{2,1,0:T(8,128)(2,1)S(1)} %slice_bitcast_fusion.11), channel_id=1, source_target_pairs={{0,1},{1,2},{2,3},{3,4},{4,5},{5,6},{6,7},{8,9},{9,10},{10,11},{11... | collective-permute-start | bytes 221192 | tf_op jit(solution)/shard_map/ppermute | solution.py:481
  123.9 10.6 %all-to-all-start.4 = ((f32[16,1,768]{2,1,0:T(1,128)}), f32[16,1,768]{2,1,0:T(1,128)}, u32[]{:S(2)}, u32[]{:S(2)}) async-start(f32[16,1,768]{2,1,0:T(1,128)} %copy-done.80), calls=%async_computation.4 | async-start | bytes 98304 | tf_op jit(solution)/shard_map/all_to_all | solution.py:471
  130.4 21.5 %collective-permute-start.13 = (bf16[2,48,384]{2,1,0:T(8,128)(2,1)}, bf16[2,48,384]{2,1,0:T(8,128)(2,1)}, u32[]{:S(2)}, u32[]{:S(2)}) collective-permute-start(bf16[2,48,384]{2,1,0:T(8,128)(2,1)} %get-tuple-element.44.pool_own_ref), channel_id=1, source_target_pairs={{1,0},{2,1},{3,2},{4,3},{5,4},{6,5},{7,6},{9,8},{10,9},{11,10},{12... | collective-permute-start | bytes 221192 | tf_op jit(solution)/shard_map/ppermute | solution.py:486
  136.0 17.3 %all-to-all-start.5 = ((f32[16,1,768]{2,1,0:T(1,128)}), f32[16,1,768]{2,1,0:T(1,128)}, u32[]{:S(2)}, u32[]{:S(2)}) async-start(f32[16,1,768]{2,1,0:T(1,128)} %broadcast_in_dim.24), calls=%async_computation.5 | async-start | bytes 98304 | tf_op jit(solution)/shard_map/all_to_all | solution.py:471
  146.9 4.3 %collective-permute-start.12 = (bf16[48,384]{1,0:T(8,128)(2,1)S(1)}, bf16[48,384]{1,0:T(8,128)(2,1)S(1)}, u32[]{:S(2)}, u32[]{:S(2)}) collective-permute-start(bf16[48,384]{1,0:T(8,128)(2,1)S(1)} %slice_bitcast_fusion.19), channel_id=1, source_target_pairs={{0,1},{1,2},{2,3},{3,4},{4,5},{5,6},{6,7},{8,9},{9,10},{10,11},{11... | collective-permute-start | bytes 110600 | tf_op jit(solution)/shard_map/ppermute | solution.py:481
  161.0 34.2 %copy-start.93 = (f32[2]{0:T(128)S(1)}, f32[2]{0:T(128)}, u32[]{:S(2)}) copy-start(f32[2]{0:T(128)} %copy-done.89) | copy-start | bytes 28
  164.3 11.7 %all-to-all-start.6 = ((f32[16,1,768]{2,1,0:T(1,128)}), f32[16,1,768]{2,1,0:T(1,128)}, u32[]{:S(2)}, u32[]{:S(2)}) async-start(f32[16,1,768]{2,1,0:T(1,128)} %copy-done.81), calls=%async_computation.6 | async-start | bytes 98304 | tf_op jit(solution)/shard_map/all_to_all | solution.py:471
  170.0 23.6 %collective-permute-start.11 = (bf16[2,48,384]{2,1,0:T(8,128)(2,1)}, bf16[2,48,384]{2,1,0:T(8,128)(2,1)}, u32[]{:S(2)}, u32[]{:S(2)}) collective-permute-start(bf16[2,48,384]{2,1,0:T(8,128)(2,1)} %get-tuple-element.75), channel_id=1, source_target_pairs={{1,0},{2,1},{3,2},{4,3},{5,4},{6,5},{7,6},{9,8},{10,9},{11,10},{12... | collective-permute-start | bytes 221192 | tf_op jit(solution)/shard_map/ppermute | solution.py:486
  171.3 22.3 %collective-permute-start.10 = (bf16[2,48,384]{2,1,0:T(8,128)(2,1)}, bf16[2,48,384]{2,1,0:T(8,128)(2,1)}, u32[]{:S(2)}, u32[]{:S(2)}) collective-permute-start(bf16[2,48,384]{2,1,0:T(8,128)(2,1)} %get-tuple-element.76), channel_id=1, source_target_pairs={{0,1},{1,2},{2,3},{3,4},{4,5},{5,6},{6,7},{8,9},{9,10},{10,11},{11... | collective-permute-start | bytes 221192 | tf_op jit(solution)/shard_map/ppermute | solution.py:481
  178.7 16.6 %all-to-all-start.7 = ((f32[16,1,768]{2,1,0:T(1,128)}), f32[16,1,768]{2,1,0:T(1,128)}, u32[]{:S(2)}, u32[]{:S(2)}) async-start(f32[16,1,768]{2,1,0:T(1,128)} %broadcast_in_dim.25), calls=%async_computation.7 | async-start | bytes 98304 | tf_op jit(solution)/shard_map/all_to_all | solution.py:471
  188.3 5.3 %collective-permute-start.15 = (bf16[48,384]{1,0:T(8,128)(2,1)S(1)}, bf16[48,384]{1,0:T(8,128)(2,1)S(1)}, u32[]{:S(2)}, u32[]{:S(2)}) collective-permute-start(bf16[48,384]{1,0:T(8,128)(2,1)S(1)} %get-tuple-element.81), channel_id=1, source_target_pairs={{1,0},{2,1},{3,2},{4,3},{5,4},{6,5},{7,6},{9,8},{10,9},{11,10},{12... | collective-permute-start | bytes 110600 | tf_op jit(solution)/shard_map/ppermute | solution.py:486
  189.6 5.0 %collective-permute-start.14 = (bf16[48,384]{1,0:T(8,128)(2,1)S(1)}, bf16[48,384]{1,0:T(8,128)(2,1)S(1)}, u32[]{:S(2)}, u32[]{:S(2)}) collective-permute-start(bf16[48,384]{1,0:T(8,128)(2,1)S(1)} %get-tuple-element.82), channel_id=1, source_target_pairs={{0,1},{1,2},{2,3},{3,4},{4,5},{5,6},{6,7},{8,9},{9,10},{10,11},{11... | collective-permute-start | bytes 110600 | tf_op jit(solution)/shard_map/ppermute | solution.py:481
  205.3 13.7 %all-to-all-start.8 = ((f32[16,1,768]{2,1,0:T(1,128)}), f32[16,1,768]{2,1,0:T(1,128)}, u32[]{:S(2)}, u32[]{:S(2)}) async-start(f32[16,1,768]{2,1,0:T(1,128)} %copy-done.84), calls=%async_computation.8 | async-start | bytes 98304 | tf_op jit(solution)/shard_map/all_to_all | solution.py:471
  212.8 26.6 %collective-permute-start.7 = (bf16[4,48,384]{2,1,0:T(8,128)(2,1)}, bf16[4,48,384]{2,1,0:T(8,128)(2,1)}, u32[]{:S(2)}, u32[]{:S(2)}) collective-permute-start(bf16[4,48,384]{2,1,0:T(8,128)(2,1)} %get-tuple-element.67), channel_id=1, source_target_pairs={{1,0},{2,1},{3,2},{4,3},{5,4},{6,5},{7,6},{9,8},{10,9},{11,10},{12... | collective-permute-start | bytes 442376 | tf_op jit(solution)/shard_map/ppermute | solution.py:486
  214.0 25.4 %collective-permute-start.6 = (bf16[4,48,384]{2,1,0:T(8,128)(2,1)}, bf16[4,48,384]{2,1,0:T(8,128)(2,1)}, u32[]{:S(2)}, u32[]{:S(2)}) collective-permute-start(bf16[4,48,384]{2,1,0:T(8,128)(2,1)} %get-tuple-element.68), channel_id=1, source_target_pairs={{0,1},{1,2},{2,3},{3,4},{4,5},{5,6},{6,7},{8,9},{9,10},{10,11},{11... | collective-permute-start | bytes 442376 | tf_op jit(solution)/shard_map/ppermute | solution.py:481
  221.8 19.7 %all-to-all-start.9 = ((f32[16,1,768]{2,1,0:T(1,128)}), f32[16,1,768]{2,1,0:T(1,128)}, u32[]{:S(2)}, u32[]{:S(2)}) async-start(f32[16,1,768]{2,1,0:T(1,128)} %broadcast_in_dim.26), calls=%async_computation.9 | async-start | bytes 98304 | tf_op jit(solution)/shard_map/all_to_all | solution.py:471
  234.1 5.7 %collective-permute-start.17 = (bf16[2,48,384]{2,1,0:T(8,128)(2,1)S(1)}, bf16[2,48,384]{2,1,0:T(8,128)(2,1)S(1)}, u32[]{:S(2)}, u32[]{:S(2)}) collective-permute-start(bf16[2,48,384]{2,1,0:T(8,128)(2,1)S(1)} %get-tuple-element.73), channel_id=1, source_target_pairs={{1,0},{2,1},{3,2},{4,3},{5,4},{6,5},{7,6},{9,8},{10,9},{11,10},{12... | collective-permute-start | bytes 221192 | tf_op jit(solution)/shard_map/ppermute | solution.py:486
  235.4 5.4 %collective-permute-start.16 = (bf16[2,48,384]{2,1,0:T(8,128)(2,1)S(1)}, bf16[2,48,384]{2,1,0:T(8,128)(2,1)S(1)}, u32[]{:S(2)}, u32[]{:S(2)}) collective-permute-start(bf16[2,48,384]{2,1,0:T(8,128)(2,1)S(1)} %get-tuple-element.74), channel_id=1, source_target_pairs={{0,1},{1,2},{2,3},{3,4},{4,5},{5,6},{6,7},{8,9},{9,10},{10,11},{11... | collective-permute-start | bytes 221192 | tf_op jit(solution)/shard_map/ppermute | solution.py:481
  254.1 32.1 %copy-start.9 = (bf16[2,4,3,3,384]{4,3,2,1,0:T(4,128)(2,1)S(1)}, bf16[2,4,3,3,384]{4,3,2,1,0:T(4,128)(2,1)}, u32[]{:S(2)}) copy-start(bf16[2,4,3,3,384]{4,3,2,1,0:T(4,128)(2,1)} %copy-done.3) | copy-start | bytes 165892
  254.1 32.1 %copy-start.33 = (f32[2,4,384]{2,1,0:T(4,128)S(1)}, f32[2,4,384]{2,1,0:T(4,128)}, u32[]{:S(2)}) copy-start(f32[2,4,384]{2,1,0:T(4,128)} %bias_ref.17) | copy-start | bytes 36868
  254.1 32.1 %copy-start.100 = (f32[18]{0:T(128)S(1)}, f32[18]{0:T(128)}, u32[]{:S(2)}) copy-start(f32[18]{0:T(128)} %copy-done.94) | copy-start | bytes 220
  254.2 32.1 %copy-start.103 = (f32[2,384]{1,0:T(2,128)S(1)}, f32[2,384]{1,0:T(2,128)}, u32[]{:S(2)}) copy-start(f32[2,384]{1,0:T(2,128)} %copy-done.101) | copy-start | bytes 9220
  254.2 12.4 %all-to-all-start.10 = ((f32[16,1,768]{2,1,0:T(1,128)}), f32[16,1,768]{2,1,0:T(1,128)S(1)}, u32[]{:S(2)}, u32[]{:S(2)}) async-start(f32[16,1,768]{2,1,0:T(1,128)} %copy-done.85), calls=%async_computation.10 | async-start | bytes 98304 | tf_op jit(solution)/shard_map/all_to_all | solution.py:471
  261.7 24.6 %collective-permute-start.19 = (bf16[2,2,48,384]{3,2,1,0:T(8,128)(2,1)S(1)}, bf16[2,2,48,384]{3,2,1,0:T(8,128)(2,1)S(1)}, u32[]{:S(2)}, u32[]{:S(2)}) collective-permute-start(bf16[2,2,48,384]{3,2,1,0:T(8,128)(2,1)S(1)} %get-tuple-element.55.pool_own_ref), channel_id=1, source_target_pairs={{1,0},{2,1},{3,2},{4,3},{5,4},{6,5},{7,6},{9,8},{10,9},{11,10},{12... | collective-permute-start | bytes 442376 | tf_op jit(solution)/shard_map/ppermute | solution.py:486
  267.3 19.0 %all-to-all-start.11 = ((f32[16,1,768]{2,1,0:T(1,128)}), f32[16,1,768]{2,1,0:T(1,128)S(1)}, u32[]{:S(2)}, u32[]{:S(2)}) async-start(f32[16,1,768]{2,1,0:T(1,128)} %broadcast_in_dim.27), calls=%async_computation.11 | async-start | bytes 98304 | tf_op jit(solution)/shard_map/all_to_all | solution.py:471
  279.2 4.7 %collective-permute-start.18 = (bf16[2,48,384]{2,1,0:T(8,128)(2,1)S(1)}, bf16[2,48,384]{2,1,0:T(8,128)(2,1)S(1)}, u32[]{:S(2)}, u32[]{:S(2)}) collective-permute-start(bf16[2,48,384]{2,1,0:T(8,128)(2,1)S(1)} %slice_bitcast_fusion.6), channel_id=1, source_target_pairs={{0,1},{1,2},{2,3},{3,4},{4,5},{5,6},{6,7},{8,9},{9,10},{10,11},{11... | collective-permute-start | bytes 221192 | tf_op jit(solution)/shard_map/ppermute | solution.py:481
  291.6 30.6 %copy-start.38 = (bf16[2,48,384]{2,1,0:T(8,128)(2,1)S(1)}, bf16[2,48,384]{2,1,0:T(8,128)(2,1)}, u32[]{:S(2)}) copy-start(bf16[2,48,384]{2,1,0:T(8,128)(2,1)} %copy-done.36) | copy-start | bytes 221188
  291.6 30.6 %copy-start.72 = (bf16[48,384]{1,0:T(8,128)(2,1)S(1)}, bf16[48,384]{1,0:T(8,128)(2,1)}, u32[]{:S(2)}) copy-start(bf16[48,384]{1,0:T(8,128)(2,1)} %copy-done.70) | copy-start | bytes 110596
  291.6 30.6 %copy-start.75 = (bf16[48,384]{1,0:T(8,128)(2,1)S(1)}, bf16[48,384]{1,0:T(8,128)(2,1)}, u32[]{:S(2)}) copy-start(bf16[48,384]{1,0:T(8,128)(2,1)} %copy-done.73) | copy-start | bytes 110596
  291.6 30.6 %copy-start.107 = (f32[2,384]{1,0:T(2,128)S(1)}, f32[2,384]{1,0:T(2,128)}, u32[]{:S(2)}) copy-start(f32[2,384]{1,0:T(2,128)} %copy-done.106) | copy-start | bytes 9220
  294.8 9.9 %all-to-all-start.12 = ((f32[16,1,768]{2,1,0:T(1,128)}), f32[16,1,768]{2,1,0:T(1,128)S(1)}, u32[]{:S(2)}, u32[]{:S(2)}) async-start(f32[16,1,768]{2,1,0:T(1,128)} %copy-done.82), calls=%async_computation.12 | async-start | bytes 98304 | tf_op jit(solution)/shard_map/all_to_all | solution.py:471
  298.4 21.0 %collective-permute-start.21 = (bf16[2,48,384]{2,1,0:T(8,128)(2,1)S(1)}, bf16[2,48,384]{2,1,0:T(8,128)(2,1)S(1)}, u32[]{:S(2)}, u32[]{:S(2)}) collective-permute-start(bf16[2,48,384]{2,1,0:T(8,128)(2,1)S(1)} %get-tuple-element.61.pool_own_ref), channel_id=1, source_target_pairs={{1,0},{2,1},{3,2},{4,3},{5,4},{6,5},{7,6},{9,8},{10,9},{11,10},{12... | collective-permute-start | bytes 221192 | tf_op jit(solution)/shard_map/ppermute | solution.py:486
  305.4 16.7 %all-to-all-start.13 = ((f32[16,1,768]{2,1,0:T(1,128)}), f32[16,1,768]{2,1,0:T(1,128)S(1)}, u32[]{:S(2)}, u32[]{:S(2)}) async-start(f32[16,1,768]{2,1,0:T(1,128)} %broadcast_in_dim.28), calls=%async_computation.13 | async-start | bytes 98304 | tf_op jit(solution)/shard_map/all_to_all | solution.py:471
  315.1 4.3 %collective-permute-start.20 = (bf16[48,384]{1,0:T(8,128)(2,1)S(1)}, bf16[48,384]{1,0:T(8,128)(2,1)S(1)}, u32[]{:S(2)}, u32[]{:S(2)}) collective-permute-start(bf16[48,384]{1,0:T(8,128)(2,1)S(1)} %slice_bitcast_fusion.16), channel_id=1, source_target_pairs={{0,1},{1,2},{2,3},{3,4},{4,5},{5,6},{6,7},{8,9},{9,10},{10,11},{11... | collective-permute-start | bytes 110600 | tf_op jit(solution)/shard_map/ppermute | solution.py:481
  322.2 19.7 %copy-start.111 = (f32[2,384]{1,0:T(2,128)S(1)}, f32[2,384]{1,0:T(2,128)}, u32[]{:S(2)}) copy-start(f32[2,384]{1,0:T(2,128)} %copy-done.110) | copy-start | bytes 9220
  333.2 15.7 %all-to-all-start.15 = ((f32[16,1,768]{2,1,0:T(1,128)}), f32[16,1,768]{2,1,0:T(1,128)S(1)}, u32[]{:S(2)}, u32[]{:S(2)}) async-start(f32[16,1,768]{2,1,0:T(1,128)} %broadcast_in_dim.29), calls=%async_computation.15 | async-start | bytes 98304 | tf_op jit(solution)/shard_map/all_to_all | solution.py:471
  (106 other events, 126.8 us)
